TPU v7x, 32 devices: a whole 2x2x4 slice. The times are simulated.
32 devices in a mesh: lon: 2 (over x), lat: 4 (over y, core), head: 4 (over z).
Axes of the slice: x: 2, y: 2, z: 4, core: 2. Of those that a mesh axis runs over, the one named last changes fastest.
Arguments:
- features: bfloat16 [8, 24, 24, 384], P(None, 'lat', 'lon'), may hold values from -6 to 6
- attend_weight: bfloat16 [3, 384, 384], P(None, None, 'head'), may hold values from -0.3125 to 0.3125
- output_weight: bfloat16 [384, 384], P('head'), may hold values from -0.3125 to 0.3125
- bias_table: float32 [64, 12, 3312], P(None, 'head'), may hold values from -3 to 304
- bias_type: int32 [4, 4], P(None, 'lat'), may hold values from 0 to 63
- window_shift: int32 [1], replicated, may hold values from 1 to 11
- grad_out: bfloat16 [8, 24, 24, 384], P(None, 'lat', 'lon'), may hold values from -6 to 6
Outputs:
- feature_grad: bfloat16 [8, 24, 24, 384], P(None, 'lat', 'lon', 'head')
- attend_grad: float32 [3, 384, 384], P(None, None, 'head')
- output_grad: float32 [384, 384], P('head')
- bias_grad: float32 [64, 12, 3312], P(None, 'head')
All inputs are finite; a program needn't handle non-finite values.
Results may differ from a plain program's by a relative error of at most 0.01.
Values may be sent and summed in bfloat16 or wider, within the bound.
A program may use at most 128 MiB of HBM per device.

v0:
```python
import functools

import jax
import jax.numpy as jnp
from jax import lax
from jax.experimental import pallas as pl
from jax.experimental.pallas import tpu as pltpu
from jax.sharding import PartitionSpec as P

WIN_LEVEL = 2
WIN_LAT = 6
WIN_LON = 12
ROWS = WIN_LEVEL * WIN_LAT
HALF = WIN_LON // 2
SPAN = 2 * WIN_LON - 1
PAD = 16
TOK = ROWS * PAD
F32 = jnp.float32
BF16 = jnp.bfloat16


def from_behind(x, axis, by):
    count = lax.axis_size(axis)
    return lax.ppermute(x, axis, [(i, (i + by) % count) for i in range(count)])


def dot(a, b, dims):
    return lax.dot_general(a, b, (dims, ((), ())), preferred_element_type=F32)


NN = ((1,), (0,))
NT = ((1,), (1,))
TN = ((0,), (0,))


def use_neighbour(shift, col):
    first = jnp.where(shift <= HALF, 0, shift)
    return (col >= first) & (col < jnp.where(shift <= HALF, shift, WIN_LON))


def spread_matrix(lanes, shift):
    row = lax.broadcasted_iota(jnp.int32, (lanes, TOK), 0)
    key = lax.broadcasted_iota(jnp.int32, (lanes, TOK), 1)
    slot = key % PAD
    pos = slot + WIN_LON - shift
    pos = jnp.where(pos >= WIN_LON, pos - WIN_LON, pos)
    hit = (row == key // PAD * SPAN + WIN_LON - 1 - pos) & (slot < WIN_LON)
    return jnp.where(hit, 1.0, 0.0).astype(BF16)


def bias_kernel(heads, shift_ref, type_ref, table_ref, bias_a, bias_b, kinds_ref, rel, table, line, sems):
    shift = shift_ref[0]
    wins = table.shape[0]
    part = WIN_LAT * SPAN
    copies = [
        pltpu.make_async_copy(table_ref.at[type_ref[w, 0]], table.at[w], sems.at[w]) for w in range(wins)
    ]
    for copy in copies:
        copy.start()

    for copy in copies:
        copy.wait()
    rel[...] = jnp.zeros_like(rel)
    line[...] = jnp.zeros_like(line)
    kinds_ref[...] = jnp.full_like(kinds_ref, -1)
    for w in range(wins):
        line[w * heads:(w + 1) * heads, :table.shape[2]] = table[w]
        kinds_ref[w * heads:(w + 1) * heads, :] = jnp.full((heads, kinds_ref.shape[1]), type_ref[w, 0], jnp.int32)
    for k in range(WIN_LEVEL * WIN_LEVEL * WIN_LAT):
        zi, zj, ai = k // (WIN_LEVEL * WIN_LAT), k // WIN_LAT % WIN_LEVEL, k % WIN_LAT
        rel[zi * WIN_LAT + ai, :, zj * part:(zj + 1) * part] = line[:, k * part:(k + 1) * part]
    lanes = rel.shape[2]
    spread = spread_matrix(lanes, shift)
    unused = jnp.where(lax.broadcasted_iota(jnp.int32, (1, TOK), 1) % PAD < WIN_LON, 0.0, -1e30)
    group = PAD
    flat = rel[...].reshape(ROWS * group, lanes)
    for c in range(PAD):
        if c < WIN_LON:
            place = lax.rem(c + WIN_LON - shift, WIN_LON)
            moved = pltpu.roll(flat, lanes - place, 1)
            one = moved.astype(BF16)
            rest = moved - one.astype(F32)
            two = rest.astype(BF16)
            three = (rest - two.astype(F32)).astype(BF16)
            out = dot(one, spread, NN) + dot(two, spread, NN) + dot(three, spread, NN) + unused
        else:
            out = jnp.zeros((ROWS * group, TOK), F32)
        for p in range(ROWS):
            base = (p * PAD + c) * group
            bias_a[base:base + group, :] = out[p * group:(p + 1) * group, :128]
            bias_b[base:base + group, :TOK - 128] = out[p * group:(p + 1) * group, 128:]


def spread_bias(bias_table, bias_type, shift):
    heads, rel_total = bias_table.shape[1:]
    wins = bias_type.shape[0]
    vmem = pl.BlockSpec(memory_space=pltpu.VMEM)
    smem = pl.BlockSpec(memory_space=pltpu.SMEM)
    lanes = -(-ROWS * SPAN // 128) * 128
    return pl.pallas_call(
        functools.partial(bias_kernel, heads),
        out_shape=(
            jax.ShapeDtypeStruct((TOK * PAD, 128), F32),
            jax.ShapeDtypeStruct((TOK * PAD, 128), F32),
            jax.ShapeDtypeStruct((PAD, 128), jnp.int32),
        ),
        in_specs=[smem, smem, pl.BlockSpec(memory_space=pl.ANY)],
        out_specs=(vmem,) * 3,
        scratch_shapes=[
            pltpu.VMEM((ROWS, PAD, lanes), F32),
            pltpu.VMEM((wins, heads, rel_total), F32),
            pltpu.VMEM((PAD, -(-rel_total // 128) * 128), F32),
            pltpu.SemaphoreType.DMA((wins,)),
        ],
        compiler_params=pltpu.CompilerParams(vmem_limit_bytes=20 * 1024 * 1024),
        cost_estimate=pl.CostEstimate(flops=5 * 10**8, bytes_accessed=4 * 10**6, transcendentals=0),
    )(shift, bias_type, bias_table)


def block_kernel(heads, shift_ref, x_ref, g_ref, low_ref, high_ref, aw_ref, ow_ref, from_a, from_b,
                 piece_ref, grad_w_ref, grad_bias_ref,
                 xs, gs, proj, gproj, att, bias_a, bias_b, rel, line, piece):
    shift = shift_ref[0]
    wins = x_ref.shape[0] // ROWS
    width = x_ref.shape[-1]
    inner = aw_ref.shape[2]
    size = inner // heads
    part = WIN_LAT * SPAN
    lines = wins * ROWS
    col = lax.broadcasted_iota(jnp.int32, (lines, WIN_LON, width), 1)
    taken = use_neighbour(shift, col)
    for src, dst, n in ((x_ref, xs, 0), (g_ref, gs, 1)):
        near = jnp.concatenate([low_ref[n].astype(F32), high_ref[n].astype(F32)], axis=1)
        picked = jnp.where(taken, near, src[...].astype(F32))
        full = jnp.concatenate([picked, jnp.zeros((lines, PAD - WIN_LON, width), F32)], axis=1)
        dst[...] = full.astype(BF16).reshape(lines * PAD, width)
    tokens = xs[...]
    grads = gs[...]
    for c in range(3):
        proj[c] = dot(tokens, aw_ref[c], NN).astype(BF16)
    proj[3] = dot(grads, ow_ref[...], NT).astype(BF16)

    spread = spread_matrix(rel.shape[2], shift)
    lanes = rel.shape[2]
    group = PAD

    scaling = size ** -0.5
    lane = lax.broadcasted_iota(jnp.int32, (TOK, inner), 1) // size
    for w in range(wins):
        span = slice(w * TOK, (w + 1) * TOK)
        q, k, v, ga = proj[0, span], proj[1, span], proj[2, span], proj[3, span]
        sums = [None] * 4
        for h in range(heads):
            e = w * heads + h
            mine = (lane == h).astype(BF16)
            qh, kh, vh, gah = q * mine, k * mine, v * mine, ga * mine
            rows = pl.ds(e, TOK, stride=group)
            bias = jnp.concatenate([from_a[rows, :], from_b[rows, :][:, :TOK - 128]], axis=1)
            scores = dot(qh, k, NT) * scaling + bias
            top = jnp.max(scores, axis=1, keepdims=True)
            raised = jnp.exp(scores - top)
            soft = raised * (1.0 / jnp.sum(raised, axis=1, keepdims=True))
            half = soft.astype(BF16)
            grad_soft = dot(gah, v, NT)
            both = soft * grad_soft
            grad_scores = both - soft * jnp.sum(both, axis=1, keepdims=True)
            bias_a[rows, :] = grad_scores[:, :128]
            bias_b[rows, :] = jnp.concatenate(
                [grad_scores[:, 128:], jnp.zeros((TOK, 256 - TOK), F32)], axis=1
            )
            gsh = grad_scores.astype(BF16)
            terms = (dot(half, vh, NN), dot(gsh, kh, NN), dot(gsh, qh, TN), dot(half, gah, TN))
            sums = [t if s is None else s + t for s, t in zip(sums, terms)]
        att[span] = sums[0].astype(BF16)
        gproj[0, span] = (sums[1] * scaling).astype(BF16)
        gproj[1, span] = (sums[2] * scaling).astype(BF16)
        gproj[2, span] = sums[3].astype(BF16)

    chunks, chunk = piece_ref.shape[0], piece_ref.shape[-1]
    for n in range(chunks):
        cols = slice(n * chunk, (n + 1) * chunk)
        piece[:, :chunk] = sum(dot(gproj[c], aw_ref[c, cols, :], NT) for c in range(3))
        for c in range(WIN_LON):
            piece_ref[n, c] = piece[pl.ds(c, lines, stride=PAD), :][:, :chunk].astype(BF16)
    grad_w = [dot(gproj[c], tokens, TN).astype(BF16) for c in range(3)]
    grad_w.append(dot(att[...], grads, TN).astype(BF16))
    shares, share = grad_w_ref.shape[0], grad_w_ref.shape[1]
    grad_w = jnp.concatenate(grad_w, axis=0)
    for j in range(shares):
        grad_w_ref[j] = grad_w[j * share:(j + 1) * share]

    line[...] = jnp.zeros_like(line)
    folded = jnp.zeros((ROWS * group, lanes), F32)
    for c in range(WIN_LON):
        place = lax.rem(c + WIN_LON - shift, WIN_LON)
        parts = []
        for p in range(ROWS):
            base = (p * PAD + c) * group
            parts.append(
                jnp.concatenate(
                    [bias_a[base:base + group, :], bias_b[base:base + group, :][:, :TOK - 128]], axis=1
                )
            )
        got = jnp.concatenate(parts, axis=0)
        one = got.astype(BF16)
        two = (got - one.astype(F32)).astype(BF16)
        folded = folded + pltpu.roll(dot(one, spread, NT) + dot(two, spread, NT), place, 1)
    rel[...] = folded.reshape(ROWS, group, lanes)
    for k in range(WIN_LEVEL * WIN_LEVEL * WIN_LAT):
        zi, zj, ai = k // (WIN_LEVEL * WIN_LAT), k // WIN_LAT % WIN_LEVEL, k % WIN_LAT
        line[:, k * part:(k + 1) * part] = rel[zi * WIN_LAT + ai, :, zj * part:(zj + 1) * part]
    strips, strip = grad_bias_ref.shape[0], grad_bias_ref.shape[2]
    for j in range(strips):
        used = lax.broadcasted_iota(jnp.int32, (PAD, strip), 0) < wins * heads
        grad_bias_ref[j] = jnp.where(used, line[:, j * strip:(j + 1) * strip], 0.0).astype(BF16)


def block_backward(features, grad_out, low, high, attend_weight, output_weight, bias, table_shape, shift):
    levels, lat_rows, lon_cols, width = features.shape
    heads, rel_total = table_shape[1:]
    inner = attend_weight.shape[2]
    wins = levels // WIN_LEVEL
    lines = wins * ROWS
    chunks = lax.axis_size("head")
    strips = lax.axis_size("lon")
    shares = strips * lax.axis_size("lat")
    strip = -(-rel_total // (128 * strips)) * 128
    vmem = pl.BlockSpec(memory_space=pltpu.VMEM)
    smem = pl.BlockSpec(memory_space=pltpu.SMEM)
    lanes = -(-ROWS * SPAN // 128) * 128
    total = lines * PAD
    return pl.pallas_call(
        functools.partial(block_kernel, heads),
        out_shape=(
            jax.ShapeDtypeStruct((chunks, WIN_LON, lines, width // chunks), BF16),
            jax.ShapeDtypeStruct((shares, 4 * inner // shares, width), BF16),
            jax.ShapeDtypeStruct((strips, PAD, strip), BF16),
        ),
        in_specs=[smem] + [vmem] * 8,
        out_specs=(vmem,) * 3,
        scratch_shapes=[
            pltpu.VMEM((total, width), BF16),
            pltpu.VMEM((total, width), BF16),
            pltpu.VMEM((4, total, inner), BF16),
            pltpu.VMEM((3, total, inner), BF16),
            pltpu.VMEM((total, inner), BF16),
            pltpu.VMEM((TOK * PAD, 128), F32),
            pltpu.VMEM((TOK * PAD, 128), F32),
            pltpu.VMEM((ROWS, PAD, lanes), F32),
            pltpu.VMEM((PAD, strips * strip), F32),
            pltpu.VMEM((total, 128), F32),
        ],
        compiler_params=pltpu.CompilerParams(vmem_limit_bytes=50 * 1024 * 1024),
        cost_estimate=pl.CostEstimate(flops=10**9, bytes_accessed=10**7, transcendentals=10**6),
    )(
        shift,
        features.reshape(lines, lon_cols, width),
        grad_out.reshape(lines, lon_cols, width),
        low,
        high,
        attend_weight,
        output_weight,
        *bias,
    )


def swap_columns(low, high, shift):
    if lax.axis_size("lon") <= 2:
        got = from_behind(jnp.where(shift <= HALF, low, high), "lon", 1)
        return got, got
    return from_behind(low, "lon", -1), from_behind(high, "lon", 1)


def exchange_kernel(shift_ref, piece_ref, w_ref, bias_ref, kinds_ref,
                    own_ref, edge_ref, all_w_ref, all_bias_ref, all_kinds_ref,
                    piece_in, w_in, bias_in, w_sum, bias_sum, edge_out, send, recv):
    lons, lats, heads = (lax.axis_size(name) for name in ("lon", "lat", "head"))
    lon, lat, head = (lax.axis_index(name) for name in ("lon", "lat", "head"))
    mine = lon * lats + lat
    pairs = [(a, b) for a in range(lons) for b in range(lats) if a or b]

    def grid_peer(a, b):
        return lax.rem(lon + a, lons), lax.rem(lat + b, lats)

    def group_peer(n):
        return lax.rem(head + n, heads)

    barrier = pltpu.get_barrier_semaphore()
    for a, b in pairs:
        x, y = grid_peer(a, b)
        pl.semaphore_signal(barrier, inc=1, device_id=(x, y, head), device_id_type=pl.DeviceIdType.MESH)
    for n in range(1, heads):
        pl.semaphore_signal(
            barrier, inc=1, device_id=(lon, lat, group_peer(n)), device_id_type=pl.DeviceIdType.MESH
        )
    pl.semaphore_wait(barrier, len(pairs) + heads - 1)
    count = [0]

    def post(src, dst, device):
        k = count[0]
        count[0] += 1
        copy = pltpu.make_async_remote_copy(
            src_ref=src, dst_ref=dst, send_sem=send.at[k], recv_sem=recv.at[k],
            device_id=device, device_id_type=pl.DeviceIdType.MESH,
        )
        copy.start()
        return copy

    bias_copies = []
    for a in range(1, lons):
        x, y = grid_peer(a, 0)
        bias_copies.append(post(bias_ref.at[x], bias_in.at[a - 1], (x, y, head)))
    w_copies = []
    for i, (a, b) in enumerate(pairs):
        x, y = grid_peer(a, b)
        w_copies.append(post(w_ref.at[x * lats + y], w_in.at[i], (x, y, head)))
    piece_copies = []
    for n in range(1, heads):
        to = group_peer(n)
        piece_copies.append(post(piece_ref.at[to], piece_in.at[n - 1], (lon, lat, to)))
    late = []
    for b in range(1, lats):
        x, y = grid_peer(0, b)
        late.append(post(kinds_ref, all_kinds_ref.at[lat], (x, y, head)))
    all_kinds_ref[pl.ds(lat, 1)] = kinds_ref[...][None]

    for copy in bias_copies:
        copy.wait_recv()
    total = bias_ref[lon].astype(F32)
    for a in range(lons - 1):
        total = total + bias_in[a].astype(F32)
    bias_sum[...] = total.astype(BF16)
    all_bias_ref[pl.ds(mine, 1)] = total.astype(BF16)[None]
    for a, b in pairs:
        x, y = grid_peer(a, b)
        late.append(post(bias_sum, all_bias_ref.at[mine], (x, y, head)))

    for copy in w_copies:
        copy.wait_recv()
    total = w_ref[mine].astype(F32)
    for i in range(len(pairs)):
        total = total + w_in[i].astype(F32)
    w_sum[...] = total.astype(BF16)
    all_w_ref[pl.ds(mine, 1)] = total.astype(BF16)[None]
    for a, b in pairs:
        x, y = grid_peer(a, b)
        late.append(post(w_sum, all_w_ref.at[mine], (x, y, head)))

    for copy in piece_copies:
        copy.wait_recv()
    total = piece_ref[head].astype(F32)
    for n in range(heads - 1):
        total = total + piece_in[n].astype(F32)
    own_ref[...] = total.astype(BF16)
    if lons <= 2:
        low = jnp.where(shift_ref[0] <= HALF, 1.0, 0.0)
        edge_out[:HALF] = (total[:HALF] * low + total[HALF:] * (1.0 - low)).astype(BF16)
    else:
        edge_out[...] = total.astype(BF16)
    sends = [(1, 0)] if lons <= 2 else [(1, 0), (lons - 1, HALF)]
    for a, first in sends:
        x, y = grid_peer(a, 0)
        late.append(post(edge_out.at[pl.ds(first, HALF)], edge_ref.at[pl.ds(first, HALF)], (x, y, head)))
    if lons <= 2:
        edge_ref[HALF:] = jnp.zeros_like(edge_out[HALF:])
    for copy in late:
        copy.wait_recv()
    for copy in bias_copies + w_copies + piece_copies + late:
        copy.wait_send()


def exchange(pieces, grad_w, grad_bias, kinds, shift):
    lons, lats, heads = (lax.axis_size(name) for name in ("lon", "lat", "head"))
    shares = lons * lats
    vmem = pl.BlockSpec(memory_space=pltpu.VMEM)
    copies = (lons - 1) + 3 * (shares - 1) + (heads - 1) + (lats - 1) + 2
    return pl.pallas_call(
        exchange_kernel,
        out_shape=(
            jax.ShapeDtypeStruct(pieces.shape[1:], BF16),
            jax.ShapeDtypeStruct(pieces.shape[1:], BF16),
            jax.ShapeDtypeStruct(grad_w.shape, BF16),
            jax.ShapeDtypeStruct((shares, *grad_bias.shape[1:]), BF16),
            jax.ShapeDtypeStruct((lats, *kinds.shape), jnp.int32),
        ),
        in_specs=[pl.BlockSpec(memory_space=pltpu.SMEM)] + [vmem] * 4,
        out_specs=(vmem,) * 5,
        scratch_shapes=[
            pltpu.VMEM((heads - 1, *pieces.shape[1:]), BF16),
            pltpu.VMEM((shares - 1, *grad_w.shape[1:]), BF16),
            pltpu.VMEM((max(lons - 1, 1), *grad_bias.shape[1:]), BF16),
            pltpu.VMEM(grad_w.shape[1:], BF16),
            pltpu.VMEM(grad_bias.shape[1:], BF16),
            pltpu.VMEM(pieces.shape[1:], BF16),
            pltpu.SemaphoreType.DMA((copies,)),
            pltpu.SemaphoreType.DMA((copies,)),
        ],
        compiler_params=pltpu.CompilerParams(
            collective_id=0, has_side_effects=True, vmem_limit_bytes=50 * 1024 * 1024
        ),
    )(shift, pieces, grad_w, grad_bias, kinds)


def finish_kernel(lats, shift_ref, own_ref, edge_ref, w_ref, bias_ref, kinds_ref,
                  feature_ref, aw_ref, ow_ref, table_ref, wide):
    shift = shift_ref[0]
    cols, lines, chunk = own_ref.shape
    for c in range(cols):
        flag = use_neighbour(shift, c).astype(F32)
        other = edge_ref[c % HALF] if lats[0] <= 2 else edge_ref[c]
        mixed = other.astype(F32) * flag + own_ref[c].astype(F32) * (1.0 - flag)
        wide[c * lines:(c + 1) * lines, :chunk] = mixed
        for a in range(WIN_LAT):
            levels = wide[pl.ds(c * lines + a, lines // WIN_LAT, stride=WIN_LAT), :]
            feature_ref[a, c] = levels[:, :chunk].astype(BF16)
    full = jnp.concatenate([w_ref[j].astype(F32) for j in range(w_ref.shape[0])], axis=0)
    inner = full.shape[0] // 4
    for c in range(3):
        aw_ref[c] = full[c * inner:(c + 1) * inner]
    ow_ref[...] = full[3 * inner:]

    rows = kinds_ref.shape[0] * kinds_ref.shape[1]
    kinds = kinds_ref[...].reshape(rows, 128)
    heads, types, total = table_ref.shape
    held = lax.broadcasted_iota(jnp.int32, (rows, 128), 0) % kinds_ref.shape[1] % heads
    lane = lax.broadcasted_iota(jnp.int32, (rows, 128), 1)
    strip = bias_ref.shape[2]
    for h in range(heads):
        pick = ((kinds == lane) & (held == h)).astype(F32).astype(BF16)[:, :types]
        for j in range(lats[0]):
            wide_rows = jnp.concatenate(
                [bias_ref[j * lats[1] + b] for b in range(lats[1])], axis=0
            )
            stop = min(total, (j + 1) * strip)
            if stop > j * strip:
                out = dot(pick, wide_rows, TN)
                table_ref[h, :, j * strip:stop] = out[:, :stop - j * strip]


def finish(own, edge, all_w, all_bias, all_kinds, shift, types, heads, rel_total):
    cols, lines, chunk = own.shape
    inner = all_w.shape[0] * all_w.shape[1] // 4
    width = all_w.shape[2]
    vmem = pl.BlockSpec(memory_space=pltpu.VMEM)
    return pl.pallas_call(
        functools.partial(finish_kernel, (lax.axis_size("lon"), lax.axis_size("lat"))),
        out_shape=(
            jax.ShapeDtypeStruct((WIN_LAT, cols, lines // WIN_LAT, chunk), BF16),
            jax.ShapeDtypeStruct((3, inner, width), F32),
            jax.ShapeDtypeStruct((inner, width), F32),
            jax.ShapeDtypeStruct((heads, types, rel_total), F32),
        ),
        in_specs=[pl.BlockSpec(memory_space=pltpu.SMEM)] + [vmem] * 5,
        out_specs=(vmem,) * 4,
        scratch_shapes=[pltpu.VMEM((lines * cols, 128), F32)],
        compiler_params=pltpu.CompilerParams(vmem_limit_bytes=50 * 1024 * 1024),
    )(shift, own, edge, all_w, all_bias, all_kinds)


def per_device(features, attend_weight, output_weight, bias_table, bias_type, window_shift, grad_out):
    shift = window_shift[0]
    levels, lat_rows, lon_cols, width = features.shape
    stored = [x.transpose(1, 2, 0, 3) for x in (features, grad_out)]
    low, high = swap_columns(
        jnp.stack([x[:, :HALF] for x in stored]), jnp.stack([x[:, HALF:] for x in stored]), shift
    )
    bias = spread_bias(bias_table, bias_type, window_shift)
    low, high = (
        x.transpose(0, 3, 1, 2, 4).reshape(2, levels * lat_rows, HALF, width) for x in (low, high)
    )
    pieces, grad_w, grad_bias = block_backward(
        features, grad_out, low, high, attend_weight, output_weight, bias[:2], bias_table.shape, window_shift
    )
    kinds = bias[2]
    gathered = exchange(pieces, grad_w, grad_bias, kinds, window_shift)
    feature_grad, attend_grad, output_grad, bias_grad = finish(*gathered, window_shift, *bias_table.shape)
    return (
        feature_grad.transpose(2, 0, 1, 3),
        attend_grad.transpose(0, 2, 1),
        output_grad,
        bias_grad.transpose(1, 0, 2),
    )


def solution(mesh):
    placed = (
        P(None, "lat", "lon", None),
        P(None, None, "head"),
        P("head", None),
        P(None, "head", None),
        P(None, "lat"),
        P(),
        P(None, "lat", "lon", None),
    )
    return jax.shard_map(
        per_device,
        mesh=mesh,
        in_specs=placed,
        out_specs=(
            P(None, "lat", "lon", "head"),
            P(None, None, "head"),
            P("head", None),
            P(None, "head", None),
        ),
        check_vma=False,
    )
```

profile of v0, /device:TPU:0, one launch (start us, length us, event | category | flops | bytes accessed | tf_op | source)
XLA Modules:
  0.0 52.8 jit_solution(14951088875869269423)
XLA Ops:
  0.6 0.0 copy-start.7
  0.6 0.0 copy-start.8
  1.4 0.0 copy-start.6
  1.4 1.5 %slice_bitcast_fusion = (bf16[1,6,6,8,384]{4,3,2,1,0:T(8,128)(2,1)S(1)}, bf16[1,6,6,8,384]{4,3,2,1,0:T(8,128)(2,1)S(1)}, bf16[1,6,6,8,384]{4,3,2,1,0:T(8,128)(2,1)S(1)}, bf16[1,6,6,8,384]{4,3,2,1,0:T(8,128)(2,1)S(1)}) fusion(bf16[6,12,8,384]{3,2,1,0:T(8,128)(2,1)} %bitcast.23, bf16[6,12,8,384]{3,2,1,0:T(8,128)(2,1)} %bitcast.22), kind=kLoop, calls=%fused_computation.1 | loop fusion | bytes 1769472 | tf_op jit(solution)/shard_map/stack | solution.py:465
  2.9 0.9 %maximum_select_fusion = bf16[2,6,6,8,384]{4,3,2,1,0:T(8,128)(2,1)} fusion(bf16[1,6,6,8,384]{4,3,2,1,0:T(8,128)(2,1)S(1)} %get-tuple-element.37, bf16[1,6,6,8,384]{4,3,2,1,0:T(8,128)(2,1)S(1)} %get-tuple-element.38, bf16[1,6,6,8,384]{4,3,2,1,0:T(8,128)(2,1)S(1)} %get-tuple-element.36, bf16[1,6,6,8,384]{4,3,2,1,0:T(8,128)(2,1)S(1)} %get-tuple-element.39, pred[]{:T(512)} %bitcast.2), kind=kLoop, calls=%fused_computation | loop fusion | flops 663552 | bytes 1327105 | tf_op jit(solution)/shard_map/jit(_where)/select_n | solution.py:269
  3.7 3.0 %collective-permute-start = (bf16[2,6,6,8,384]{4,3,2,1,0:T(8,128)(2,1)}, bf16[2,6,6,8,384]{4,3,2,1,0:T(8,128)(2,1)}, u32[]{:S(2)}, u32[]{:S(2)}) collective-permute-start(bf16[2,6,6,8,384]{4,3,2,1,0:T(8,128)(2,1)} %maximum_select_fusion), channel_id=1, source_target_pairs={{0,16},{16,0},{1,17},{17,1},{2,18},{18,2},{3,19},{19,3},{4,20},{20... | collective-permute-start | bytes 1327112 | tf_op jit(solution)/shard_map/ppermute | solution.py:24
  6.7 0.0 copy-done.7
  6.7 0.9 %copy.11 = bf16[8,6,12,384]{3,2,1,0:T(8,128)(2,1)} copy(bf16[8,6,12,384]{3,0,2,1:T(8,128)(2,1)S(1)} %copy-done.7) | data formatting | bytes 884736 | tf_op args[0]
  7.6 0.0 copy-done.8
  7.6 0.9 %copy.12 = bf16[8,6,12,384]{3,2,1,0:T(8,128)(2,1)} copy(bf16[8,6,12,384]{3,0,2,1:T(8,128)(2,1)S(1)} %copy-done.8) | data formatting | bytes 884736 | tf_op args[6]
  8.5 0.0 copy-done.6
  8.5 0.0 copy-start.9
  8.5 1.8 %copy.15.table_ref = f32[64,3,3312]{2,1,0:T(4,128)S(1)} copy(f32[64,3,3312]{2,0,1:T(8,128)S(1)} %copy-done.6) | data formatting | bytes 5087232 | tf_op args[3]
  10.3 0.0 copy-done.9
  10.3 0.0 copy-start.5
  10.3 0.1 copy.14.type_ref
  10.4 1.8 %copy.16.aw_ref = bf16[3,384,96]{2,1,0:T(8,128)(2,1)} copy(bf16[3,384,96]{1,2,0:T(8,128)(2,1)} %param.8) | data formatting | bytes 442368 | tf_op args[1]
  12.2 0.0 copy-start
  12.2 0.0 copy-start.1
  12.2 0.0 copy-start.4
  12.2 3.5 %shard_map.102 = (f32[3072,128]{1,0:T(8,128)S(1)}, f32[3072,128]{1,0:T(8,128)S(1)}, s32[16,128]{1,0:T(8,128)S(1)}) custom-call(s32[1]{0:T(128)S(6)} %copy.17.shift_ref, s32[4,1]{1,0:T(4,128)S(1)} %copy.14.type_ref, f32[64,3,3312]{2,1,0:T(4,128)S(1)} %copy.15.table_ref), custom_call_target="tpu_custom_call" | custom-call | flops 500000000 | bytes 4000000 | tf_op jit(solution)/shard_map/pallas_call | solution.py:100
  15.8 0.0 copy-start.2
  15.8 1.1 %copy-done.2 = f32[3072,128]{1,0:T(8,128)} copy-done((f32[3072,128]{1,0:T(8,128)}, f32[3072,128]{1,0:T(8,128)S(1)}, u32[]{:S(2)}) %copy-start.2) | copy-done | bytes 1572888
  16.9 0.0 copy-start.3
  16.9 1.2 %copy-done.3 = f32[3072,128]{1,0:T(8,128)} copy-done((f32[3072,128]{1,0:T(8,128)}, f32[3072,128]{1,0:T(8,128)S(1)}, u32[]{:S(2)}) %copy-start.3) | copy-done | bytes 1572888
  18.1 0.0 collective-permute-done
  18.1 1.1 %copy.13 = bf16[2,8,6,6,384]{4,3,2,1,0:T(8,128)(2,1)S(1)} copy(bf16[2,8,6,6,384]{4,1,3,2,0:T(8,128)(2,1)} %bitcast.9) | data formatting | bytes 884736 | tf_op jit(solution)/shard_map/transpose | solution.py:469
  19.2 0.0 copy-done.5
  19.2 0.0 copy-done
  19.2 0.0 copy-done.1
  19.2 0.0 copy-done.4
  19.3 11.6 %shard_map.103 = (bf16[4,12,48,96]{3,2,1,0:T(8,128)(2,1)S(1)}, bf16[8,48,384]{2,1,0:T(8,128)(2,1)S(1)}, bf16[2,16,1664]{2,1,0:T(8,128)(2,1)S(1)}) custom-call(s32[1]{0:T(128)S(6)} %copy.17.shift_ref, bf16[48,12,384]{2,1,0:T(8,128)(2,1)S(1)} %bitcast.20, bf16[48,12,384]{2,1,0:T(8,128)(2,1)S(1)} %bitcast.21, bf16[2,48,6,384]{3,2,1,0:T(8,128)(2,1)S(1)} %bitcast.18, ...), custom_call_target="tpu_custom_call" | custom-call | flops 1000000000 | bytes 10000000 | tf_op jit(solution)/shard_map/pallas_call | solution.py:232
  30.8 19.7 %shard_map.104 = (bf16[12,48,96]{2,1,0:T(8,128)(2,1)S(1)}, bf16[12,48,96]{2,1,0:T(8,128)(2,1)S(1)}, bf16[8,48,384]{2,1,0:T(8,128)(2,1)S(1)}, bf16[8,16,1664]{2,1,0:T(8,128)(2,1)S(1)}, s32[4,16,128]{2,1,0:T(8,128)S(1)}) custom-call(s32[1]{0:T(128)S(6)} %copy.17.shift_ref, bf16[4,12,48,96]{3,2,1,0:T(8,128)(2,1)S(1)} %get-tuple-element.21.piece_ref, ...), custom_call_target="tpu_custom_call" | custom-call | tf_op jit(solution)/shard_map/pallas_call | solution.py:377
  50.6 2.2 %shard_map.105 = (bf16[6,12,8,96]{3,2,1,0:T(8,128)(2,1)}, f32[3,96,384]{2,1,0:T(8,128)}, f32[96,384]{1,0:T(8,128)}, f32[3,64,3312]{2,1,0:T(8,128)}) custom-call(s32[1]{0:T(128)S(6)} %copy.17.shift_ref, bf16[12,48,96]{2,1,0:T(8,128)(2,1)S(1)} %get-tuple-element.25.own_ref, bf16[12,48,96]{2,1,0:T(8,128)(2,1)S(1)} %get-tuple-element.26.edge_ref, ...), custom_call_target="tpu_custom_call" | custom-call | tf_op jit(solution)/shard_map/pallas_call | solution.py:445
Async XLA Ops:
  0.6 6.1 %copy-start.7 = (bf16[8,6,12,384]{3,0,2,1:T(8,128)(2,1)S(1)}, bf16[8,6,12,384]{3,0,2,1:T(8,128)(2,1)}, u32[]{:S(2)}) copy-start(bf16[8,6,12,384]{3,0,2,1:T(8,128)(2,1)} %param.7) | copy-start | bytes 1327108
  0.6 7.0 %copy-start.8 = (bf16[8,6,12,384]{3,0,2,1:T(8,128)(2,1)S(1)}, bf16[8,6,12,384]{3,0,2,1:T(8,128)(2,1)}, u32[]{:S(2)}) copy-start(bf16[8,6,12,384]{3,0,2,1:T(8,128)(2,1)} %param.13) | copy-start | bytes 1327108
  1.4 7.2 %copy-start.6 = (f32[64,3,3312]{2,0,1:T(8,128)S(1)}, f32[64,3,3312]{2,0,1:T(8,128)}, u32[]{:S(2)}) copy-start(f32[64,3,3312]{2,0,1:T(8,128)} %param.10) | copy-start | bytes 7630852
  3.7 14.4 %collective-permute-start = (bf16[2,6,6,8,384]{4,3,2,1,0:T(8,128)(2,1)}, bf16[2,6,6,8,384]{4,3,2,1,0:T(8,128)(2,1)}, u32[]{:S(2)}, u32[]{:S(2)}) collective-permute-start(bf16[2,6,6,8,384]{4,3,2,1,0:T(8,128)(2,1)} %maximum_select_fusion), channel_id=1, source_target_pairs={{0,16},{16,0},{1,17},{17,1},{2,18},{18,2},{3,19},{19,3},{4,20},{20... | collective-permute-start | bytes 1327112 | tf_op jit(solution)/shard_map/ppermute | solution.py:24
  8.5 1.8 %copy-start.9 = (s32[4,1]{0,1:T(1,128)S(1)}, s32[4,1]{0,1:T(1,128)}, u32[]{:S(2)}) copy-start(s32[4,1]{0,1:T(1,128)} %param.11) | copy-start | bytes 52
  10.3 8.9 %copy-start.5 = (bf16[96,384]{1,0:T(8,128)(2,1)S(1)}, bf16[96,384]{1,0:T(8,128)(2,1)}, u32[]{:S(2)}) copy-start(bf16[96,384]{1,0:T(8,128)(2,1)} %ow_ref.1) | copy-start | bytes 221188
  12.2 7.0 %copy-start = (bf16[8,6,12,384]{3,2,1,0:T(8,128)(2,1)S(1)}, bf16[8,6,12,384]{3,2,1,0:T(8,128)(2,1)}, u32[]{:S(2)}) copy-start(bf16[8,6,12,384]{3,2,1,0:T(8,128)(2,1)} %copy.11) | copy-start | bytes 1327108
  12.2 7.0 %copy-start.1 = (bf16[8,6,12,384]{3,2,1,0:T(8,128)(2,1)S(1)}, bf16[8,6,12,384]{3,2,1,0:T(8,128)(2,1)}, u32[]{:S(2)}) copy-start(bf16[8,6,12,384]{3,2,1,0:T(8,128)(2,1)} %copy.12) | copy-start | bytes 1327108
  12.2 7.0 %copy-start.4 = (bf16[3,384,96]{2,1,0:T(8,128)(2,1)S(1)}, bf16[3,384,96]{2,1,0:T(8,128)(2,1)}, u32[]{:S(2)}) copy-start(bf16[3,384,96]{2,1,0:T(8,128)(2,1)} %copy.16.aw_ref) | copy-start | bytes 663556
  15.8 1.1 %copy-start.2 = (f32[3072,128]{1,0:T(8,128)}, f32[3072,128]{1,0:T(8,128)S(1)}, u32[]{:S(2)}) copy-start(f32[3072,128]{1,0:T(8,128)S(1)} %get-tuple-element.19.from_a) | copy-start | bytes 4718596
  16.9 1.2 %copy-start.3 = (f32[3072,128]{1,0:T(8,128)}, f32[3072,128]{1,0:T(8,128)S(1)}, u32[]{:S(2)}) copy-start(f32[3072,128]{1,0:T(8,128)S(1)} %get-tuple-element.20.from_b) | copy-start | bytes 4718596
where the time goes:
time: 53.1 us; the launch traced here: 52.8 us
  Pallas kernels  37.1 us (70%)
  local copies, waits for them, and re-layouts  10.4 us (20%)
  starting transfers between devices  2.97 us (6%)
  between operations  1.47 us (3%)
  other arithmetic  0.85 us (2%)
    pallas_call x1, Pallas kernels, exchange(): pl.pallas_call(exchange_kernel, out_shape=(jax.ShapeDtypeStruct(pieces.sh...  19.7 us
    pallas_call x1, Pallas kernels, block_backward(): pl.pallas_call(functools.partial(block_kernel, heads), out_shape=(jax.Sha...  11.6 us
    unnamed x25, local copies, waits for them, and re-layouts  7.82 us
    pallas_call x1, Pallas kernels, spread_bias(): pl.pallas_call(functools.partial(bias_kernel, heads), out_shape=(jax.Shap...  3.55 us
    ppermute x1, starting transfers between devices, from_behind(): return lax.ppermute(x, axis, [(i, (i + by) % count) for i in range(count)])  2.97 us
    pallas_call x1, Pallas kernels, finish(): pl.pallas_call(functools.partial(finish_kernel, (lax.axis_size('lon'), la...  2.2 us
    another operation x1, local copies, waits for them, and re-layouts, per_device(): jnp.stack([x[:, HALF:] for x in stored])  1.5 us
    transpose x1, local copies, waits for them, and re-layouts, per_device(): x.transpose(0, 3, 1, 2, 4).reshape(2, levels * lat_rows, HALF, width)  1.1 us
  transfers between devices with their start and end apart: 1, of which 0 were waited for; matrix products, arithmetic and copies ran while one was open for 10% of the time, Pallas kernels for 7%

commit v1 on v0

v1 whole, which is shorter than its diff:
```python
import functools

import jax
import jax.numpy as jnp
from jax import lax
from jax.experimental import pallas as pl
from jax.experimental.pallas import tpu as pltpu
from jax.sharding import PartitionSpec as P

WIN_LEVEL = 2
WIN_LAT = 6
WIN_LON = 12
HALF = WIN_LON // 2
SPAN = 2 * WIN_LON - 1
SIDE = WIN_LON * WIN_LAT
TOK = WIN_LEVEL * SIDE
EDGE = HALF * WIN_LAT
MAIN = TOK - EDGE
PART = WIN_LAT * SPAN
LOG2E = 1.4426950408889634
F32 = jnp.float32
BF16 = jnp.bfloat16

NN = ((1,), (0,))
NT = ((1,), (1,))
TN = ((0,), (0,))


def dot(a, b, dims):
    return lax.dot_general(a, b, (dims, ((), ())), preferred_element_type=F32)


def up(n, to):
    return -(-n // to) * to


def bits_of(n):
    return [1 << k for k in range(n.bit_length() - 1)]


def flip(i, bit):
    return i + bit - 2 * bit * lax.rem(i // bit, 2)


def permutation():
    row = lax.broadcasted_iota(jnp.int32, (PART, 256), 0)
    out = lax.broadcasted_iota(jnp.int32, (PART, 256), 1)
    a, d = row // SPAN, row % SPAN
    place = jnp.where(d < WIN_LON, d * WIN_LAT + a, 128 + (d - WIN_LON) * WIN_LAT + a)
    return jnp.where(place == out, 1.0, 0.0).astype(BF16)


def lane_lon(lanes):
    return lax.broadcasted_iota(jnp.int32, (1, lanes), 1) % SIDE // WIN_LAT


def block_kernel(heads, shift_ref, type_ref, x_hbm, g_hbm, aw_hbm, ow_hbm, table_hbm,
                 own_ref, edge_ref, all_w_ref, all_bias_ref,
                 x_own, g_own, aw, ow, table, halo_f, own_f, halo_out, halo_in, xs, gs,
                 line, parts, bias, gbias, gp, aw_split, piece_out, piece_in, edge_out,
                 w_core, w_core_in, w_cur, w_in, bias_cur, bias_in,
                 local, halo_sem, piece_sem, edge_sem, w_sem, bias_sem):
    lons, lats, groups = (lax.axis_size(name) for name in ("lon", "lat", "head"))
    lon, lat, head = (lax.axis_index(name) for name in ("lon", "lat", "head"))
    shift = shift_ref[0]
    early = shift <= HALF
    cols, levels, width = x_own.shape[1:]
    wins = levels // WIN_LEVEL
    inner = aw.shape[1]
    size = inner // heads
    total = heads * TOK
    lanes = up(total, 128)
    tiles = lanes // 128

    loads = [
        pltpu.make_async_copy(src, dst, local.at[i])
        for i, (src, dst) in enumerate(
            ((x_hbm, x_own), (g_hbm, g_own), (table_hbm, table), (aw_hbm, aw), (ow_hbm, ow))
        )
    ]
    for load in loads:
        load.start()

    east = (lax.rem(lon + 1, lons), lat, head)
    west = (lax.rem(lon + lons - 1, lons), lat, head)
    lon_bits, lat_bits = bits_of(lons), bits_of(lats)
    mates = [(flip(lon, b), lat, head) for b in lon_bits]
    rows_up = [(lon, flip(lat, b), head) for b in lat_bits]
    sides = [east] if lons <= 2 else [east, west]
    peers = [(lon, lat, lax.rem(head + n, groups)) for n in range(1, groups)]
    greet = sides + (mates if lons > 2 else []) + rows_up + peers
    barrier = pltpu.get_barrier_semaphore()
    for device in greet:
        pl.semaphore_signal(barrier, inc=1, device_id=device, device_id_type=pl.DeviceIdType.MESH)

    def remote(src, dst, sems, k, device):
        return pltpu.make_async_remote_copy(
            src_ref=src, dst_ref=dst, send_sem=sems.at[0, k], recv_sem=sems.at[1, k],
            device_id=device, device_id_type=pl.DeviceIdType.MESH,
        )

    strips = width // 128

    def put(dst, i, spot, value):
        value = value.astype(F32)
        for t in range(strips):
            dst[i, t, spot * levels:(spot + 1) * levels, :] = value[:, t * 128:(t + 1) * 128]

    def take(src, i, level, count):
        rows = pl.ds(level, count, stride=levels)
        return jnp.concatenate([src[i, t, rows, :] for t in range(strips)], axis=1)

    loads[0].wait()
    loads[1].wait()
    sent = []
    for n in range(len(sides)):
        for i, src in enumerate((x_own, g_own)):
            for b in range(HALF):
                low = jnp.maximum(shift + b - HALF, 0)
                high = jnp.minimum(shift + b, cols - 1)
                if lons <= 2:
                    col = jnp.where(early, low, high)
                else:
                    col = high if n == 0 else low
                for a in range(WIN_LAT):
                    put(halo_f, i, b * WIN_LAT + a, src[a, col])
        for w in range(wins):
            for i in range(2):
                rows = [take(halo_f, i, WIN_LEVEL * w + z, EDGE) for z in range(WIN_LEVEL)]
                halo_out[n, w, i * 2 * EDGE:(i + 1) * 2 * EDGE, :] = jnp.concatenate(rows, axis=0).astype(BF16)
    pl.semaphore_wait(barrier, len(greet))
    for w in range(wins):
        for n, device in enumerate(sides):
            copy = remote(halo_out.at[n, w], halo_in.at[n, w], halo_sem, w * len(sides) + n, device)
            copy.start()
            sent.append(copy)

    for i, src in enumerate((x_own, g_own)):
        for b in range(WIN_LON):
            col = jnp.where(early, jnp.minimum(shift + b, cols - 1), jnp.maximum(shift + b - WIN_LON, 0))
            for a in range(WIN_LAT):
                put(own_f, i, b * WIN_LAT + a, src[a, col])

    loads[2].wait()
    parts[...] = jnp.zeros_like(parts)
    for h in range(heads):
        for w in range(wins):
            line[h * wins + w:h * wins + w + 1, :table.shape[2]] = table[h, pl.ds(type_ref[0, w], 1), :]
    block = WIN_LEVEL * WIN_LAT * wins
    spots = []
    for k in range(WIN_LEVEL * WIN_LEVEL * WIN_LAT * WIN_LAT):
        zi, zj = k // (WIN_LEVEL * WIN_LAT * WIN_LAT), k // (WIN_LAT * WIN_LAT) % WIN_LEVEL
        ai, aj = k // WIN_LAT % WIN_LAT, k % WIN_LAT
        for h in range(heads):
            seg = h * WIN_LEVEL + zi
            spots.append((k, h, seg * block + (zj * WIN_LAT + aj) * wins, ai * SPAN))
    for k, h, r, c in spots:
        parts[r:r + wins, c:c + SPAN] = line[h * wins:(h + 1) * wins, k * SPAN:(k + 1) * SPAN]
    perm = permutation()
    flat = parts[:, :PART]
    one = flat.astype(BF16)
    rest = flat - one.astype(F32)
    two = rest.astype(BF16)
    three = (rest - two.astype(F32)).astype(BF16)
    spread = (dot(one, perm, NN) + dot(two, perm, NN) + dot(three, perm, NN)) * LOG2E
    segs = heads * WIN_LEVEL
    pad = jnp.zeros((block, lanes - total), F32)

    def gathered(start):
        pieces = [spread[s * block:(s + 1) * block, start:start + SIDE] for s in range(segs)]
        return jnp.concatenate(pieces + [pad], axis=1)

    lower, upper = gathered(0), gathered(128)
    place = lane_lon(lanes)
    half = WIN_LAT * wins
    for b in range(WIN_LON):
        left = (lanes - WIN_LAT * (WIN_LON - 1 - b)) % lanes
        both = jnp.where(
            place <= b, pltpu.roll(lower, left, 1), pltpu.roll(upper, WIN_LAT * (b + 1), 1)
        )
        for z in range(WIN_LEVEL):
            r = (z * WIN_LON + b) * half
            for t in range(tiles):
                bias[t, r:r + half, :] = both[z * half:(z + 1) * half, t * 128:(t + 1) * 128]

    loads[3].wait()
    loads[4].wait()
    for c in range(3):
        for g in range(groups):
            chunk = aw[c, :, g * inner:(g + 1) * inner]
            aw_split[c, :, g * 128:(g + 1) * 128] = jnp.concatenate(
                [chunk, jnp.zeros((inner, 128 - inner), BF16)], axis=1
            )

    key_lon = lax.broadcasted_iota(jnp.int32, (TOK, 1), 0) % SIDE // WIN_LAT
    mine = jnp.where(early, (key_lon + shift < WIN_LON).astype(F32), (key_lon + shift >= WIN_LON).astype(F32)) > 0.5
    diag = (
        lax.broadcasted_iota(jnp.int32, (inner, lanes), 0) // size
        == lax.broadcasted_iota(jnp.int32, (inner, lanes), 1) // TOK
    )
    col_head = lax.broadcasted_iota(jnp.int32, (TOK, inner), 1) // size
    scaling = size ** -0.5

    def expanded(rows):
        rows = rows.astype(BF16).astype(F32)
        filled = jnp.concatenate([rows] * heads + [jnp.zeros((inner, lanes - total), F32)], axis=1)
        return jnp.where(diag, filled, 0.0).astype(BF16)

    def folded(wide_rows):
        out = jnp.zeros((TOK, inner), F32)
        for h in range(heads):
            out = jnp.where(col_head == h, wide_rows[h * TOK:(h + 1) * TOK], out)
        return out

    piece_copies = []

    def window(w):
        span = slice(w * TOK, (w + 1) * TOK)
        for n in range(len(sides)):
            sent[w * len(sides) + n].wait_recv()
        for i, dst in enumerate((xs, gs)):
            kept = [take(own_f, i, WIN_LEVEL * w + z, SIDE) for z in range(WIN_LEVEL)]
            kept = jnp.concatenate(kept, axis=0)
            near = [halo_in[n, w, i * 2 * EDGE:(i + 1) * 2 * EDGE, :].astype(F32) for n in range(len(sides))]
            first, last = (near[0], near[0]) if lons <= 2 else (near[0], near[1])
            filled = jnp.concatenate([first[:EDGE], last[:EDGE], first[EDGE:], last[EDGE:]], axis=0)
            dst[span, :] = jnp.where(mine, kept, filled).astype(BF16)
        tokens, grads = xs[span, :], gs[span, :]
        queries = expanded(dot(aw[0], tokens, NT))
        keys = dot(tokens, aw[1], NT).astype(BF16)
        values = dot(tokens, aw[2], NT).astype(BF16)
        gates = expanded(dot(ow[...], grads, NT))
        rows = pl.ds(w, TOK, stride=wins)
        offset = jnp.concatenate([bias[t, rows, :] for t in range(tiles)], axis=1)
        scores = dot(keys, queries, NN) * (scaling * LOG2E) + offset
        top = jnp.max(scores, axis=0, keepdims=True)
        raised = jnp.exp2(scores - top)
        soft = raised * (1.0 / jnp.sum(raised, axis=0, keepdims=True))
        soft_half = soft.astype(BF16)
        both = soft * dot(values, gates, NN)
        slopes = both - soft * jnp.sum(both, axis=0, keepdims=True)
        for t in range(tiles):
            gbias[t, rows, :] = slopes[:, t * 128:(t + 1) * 128]
        slopes_half = slopes.astype(BF16)
        gp[0, span, :] = (folded(dot(slopes_half, keys, TN)) * scaling).astype(BF16)
        gp[1, span, :] = (dot(slopes_half, queries, NT) * scaling).astype(BF16)
        gp[2, span, :] = dot(soft_half, gates, NT).astype(BF16)
        gp[3, span, :] = folded(dot(soft_half, values, TN)).astype(BF16)

    def send_pieces(w):
        span = slice(w * TOK, (w + 1) * TOK)
        out = sum(dot(gp[c, span, :], aw_split[c], NN) for c in range(3))
        for g in range(groups):
            chunk = out[:, g * 128:g * 128 + inner]
            tail = chunk[MAIN:]
            third = 128 - inner
            extra = jnp.concatenate([tail[:, t * third:(t + 1) * third] for t in range(inner // third)], axis=0)
            packed = jnp.concatenate([chunk[:MAIN], extra], axis=1).astype(BF16)
            piece_out[w, g, :MAIN, :] = packed
        for n, device in enumerate(peers):
            copy = remote(
                piece_out.at[w, device[2]], piece_in.at[w, n], piece_sem, w * len(peers) + n, device
            )
            copy.start()
            piece_copies.append(copy)

    edge_copies = []

    def sum_pieces(w):
        for n in range(len(peers)):
            piece_copies[w * len(peers) + n].wait_recv()
        got = piece_out[w, head].astype(F32)
        for n in range(len(peers)):
            got = got + piece_in[w, n].astype(F32)
        third = 128 - inner
        tail = [got[t * EDGE:(t + 1) * EDGE, inner:] for t in range(inner // third)]
        full = jnp.concatenate([got[:MAIN, :inner], jnp.concatenate(tail, axis=1)], axis=0)
        own_ref[w] = full.astype(BF16)
        first = jnp.concatenate([full[:EDGE], full[SIDE:SIDE + EDGE]], axis=0)
        last = jnp.concatenate([full[EDGE:SIDE], full[SIDE + EDGE:]], axis=0)
        if lons <= 2:
            outs = [jnp.where(early, last, first)]
        else:
            outs = [last, first]
        for n, device in enumerate(sides):
            edge_out[n, w] = outs[n].astype(BF16)
            copy = remote(edge_out.at[n, w], edge_ref.at[n, w], edge_sem, w * len(sides) + n, device)
            copy.start()
            edge_copies.append(copy)

    for w in range(wins):
        window(w)
        send_pieces(w)
        if w >= 2:
            sum_pieces(w - 2)

    grad_w = [dot(gp[c], xs[...], TN) for c in range(3)] + [dot(gp[3], gs[...], TN)]
    rows_w = 4 * inner
    part_w = rows_w // 2
    for c in range(4):
        first = c * inner
        w_core[first // part_w, first % part_w:first % part_w + inner, :] = grad_w[c].astype(BF16)
    count_w = [0]
    w_copies = []

    def post_w(src, dst, device):
        copy = remote(src, dst, w_sem, count_w[0], device)
        count_w[0] += 1
        copy.start()
        w_copies.append(copy)
        return copy

    keep = lax.rem(lat, 2)
    core_mate = rows_up[0]
    swap = post_w(w_core.at[1 - keep], w_core_in, core_mate)

    low_sum = jnp.zeros((block, lanes), F32)
    high_sum = jnp.zeros((block, lanes), F32)
    for b in range(WIN_LON):
        got = jnp.concatenate(
            [
                jnp.concatenate([gbias[t, (z * WIN_LON + b) * half:(z * WIN_LON + b + 1) * half, :] for t in range(tiles)], axis=1)
                for z in range(WIN_LEVEL)
            ],
            axis=0,
        )
        right = WIN_LAT * (WIN_LON - 1 - b)
        low_sum = low_sum + pltpu.roll(jnp.where(place <= b, got, 0.0), right, 1)
        high_sum = high_sum + pltpu.roll(jnp.where(place > b, got, 0.0), lanes - WIN_LAT * (b + 1), 1)

    swap.wait_recv()
    sub = part_w // 2
    orders = [
        [(b, m) for b, m in zip(lon_bits, mates)] + [(b, m) for b, m in zip(lat_bits[1:], rows_up[1:])],
        [(b, m) for b, m in zip(lat_bits[1:], rows_up[1:])] + [(b, m) for b, m in zip(lon_bits, mates)],
    ]
    steps = len(orders[0])
    flying = [None, None]
    for j in range(2):
        part = slice(j * sub, (j + 1) * sub)
        w_cur[0, j] = (w_core[keep, part, :].astype(F32) + w_core_in[part, :].astype(F32)).astype(BF16)
        flying[j] = post_w(w_cur.at[0, j], w_in.at[0, j], orders[j][0][1])

    gap = jnp.zeros((block, 128 - SIDE), F32)
    sums = jnp.concatenate(
        [
            jnp.concatenate(
                [low_sum[:, s * SIDE:(s + 1) * SIDE], gap, high_sum[:, s * SIDE:(s + 1) * SIDE], gap], axis=1
            )
            for s in range(segs)
        ],
        axis=0,
    ).astype(BF16)
    parts[:, :PART] = dot(sums, perm, NT)
    for k, h, r, c in spots:
        line[h * wins:(h + 1) * wins, k * SPAN:(k + 1) * SPAN] = parts[r:r + wins, c:c + SPAN]
    used = lax.broadcasted_iota(jnp.int32, line.shape, 0) < heads * wins
    inside = lax.broadcasted_iota(jnp.int32, line.shape, 1) < table.shape[2]
    bias_cur[0] = jnp.where(used & inside, line[...], 0.0).astype(BF16)
    count_b = [0]
    bias_copies = []

    def post_b(src, dst, device):
        copy = remote(src, dst, bias_sem, count_b[0], device)
        count_b[0] += 1
        copy.start()
        bias_copies.append(copy)
        return copy

    bias_step = post_b(bias_cur.at[0], bias_in.at[0], mates[0])

    for w in range(max(wins - 2, 0), wins):
        if w == wins - 1:
            break
        sum_pieces(w)

    def w_step(k):
        for j in range(2):
            flying[j].wait_recv()
            fresh = (w_cur[k, j].astype(F32) + w_in[k, j].astype(F32)).astype(BF16)
            w_cur[k + 1, j] = fresh
            if k + 1 < steps:
                flying[j] = post_w(w_cur.at[k + 1, j], w_in.at[k + 1, j], orders[j][k + 1][1])

    def bias_sum(k):
        bias_copies[k].wait_recv()
        fresh = bias_cur[k].astype(F32) + bias_in[k].astype(F32)
        if k + 1 < len(lon_bits):
            bias_cur[k + 1] = fresh.astype(BF16)
            post_b(bias_cur.at[k + 1], bias_in.at[k + 1], mates[k + 1])
        else:
            kind_row = lax.broadcasted_iota(jnp.int32, line.shape, 0) % wins
            kind = jnp.zeros(line.shape, F32)
            for w in range(wins):
                kind = jnp.where(kind_row == w, type_ref[0, w].astype(F32), kind)
            bias_cur[k + 1] = jnp.where(inside, fresh, kind).astype(BF16)
            all_bias_ref[pl.ds(lat, 1)] = bias_cur[k + 1][None]

    for k in range(len(lon_bits)):
        bias_sum(k)
    final = bias_cur.at[len(lon_bits)]
    spread_copies = []
    have = [lat]
    order = list(reversed(list(zip(lat_bits, rows_up))))
    for i, (b, device) in enumerate(order):
        for slot in have:
            src = final if slot is lat else all_bias_ref.at[slot]
            spread_copies.append(post_b(src, all_bias_ref.at[slot], device))
        have = have + [flip(slot, b) for slot in have]
        if i == 0:
            w_step(0)
            sum_pieces(wins - 1)
        if i + 1 < len(order):
            for copy in spread_copies:
                copy.wait_recv()
            spread_copies = []
    for k in range(1, steps):
        w_step(k)
    both_w = [
        post_w(w_cur.at[steps, j], all_w_ref.at[keep, pl.ds(j * sub, sub)], core_mate) for j in range(2)
    ]
    for j in range(2):
        all_w_ref[pl.ds(keep, 1), j * sub:(j + 1) * sub, :] = w_cur[steps, j][None]
    for copy in both_w + spread_copies + edge_copies:
        copy.wait_recv()
    for copy in sent + piece_copies + edge_copies + w_copies + bias_copies:
        copy.wait_send()


def block_backward(x, g, aw, ow, table, types, shift):
    lats_in, cols, levels, width = x.shape
    inner = aw.shape[1]
    heads, _, rel_total = table.shape
    lons, lats, groups = (lax.axis_size(name) for name in ("lon", "lat", "head"))
    wins = levels // WIN_LEVEL
    sides = 1 if lons <= 2 else 2
    lanes = up(heads * TOK, 128)
    tiles = lanes // 128
    block = WIN_LEVEL * WIN_LAT * wins
    rows = up(heads * wins, 16)
    long = up(rel_total + 1, 128)
    lon_steps = len(bits_of(lons))
    steps = lon_steps + len(bits_of(lats)) - 1
    packed = up(MAIN, 16)
    vmem = pl.BlockSpec(memory_space=pltpu.VMEM)
    smem = pl.BlockSpec(memory_space=pltpu.SMEM)
    hbm = pl.BlockSpec(memory_space=pltpu.HBM)
    dma = pltpu.SemaphoreType.DMA
    return pl.pallas_call(
        functools.partial(block_kernel, heads),
        out_shape=(
            pltpu.VMEM((wins, TOK, inner), BF16),
            pltpu.VMEM((sides, wins, 2 * EDGE, inner), BF16),
            pltpu.VMEM((2, 2 * inner, width), BF16),
            pltpu.VMEM((lats, rows, long), BF16),
        ),
        in_specs=[smem, smem] + [hbm] * 5,
        out_specs=(vmem,) * 4,
        scratch_shapes=[
            pltpu.VMEM(x.shape, BF16),
            pltpu.VMEM(g.shape, BF16),
            pltpu.VMEM(aw.shape, BF16),
            pltpu.VMEM(ow.shape, BF16),
            pltpu.VMEM(table.shape, F32),
            pltpu.VMEM((2, width // 128, EDGE * levels, 128), F32),
            pltpu.VMEM((2, width // 128, SIDE * levels, 128), F32),
            pltpu.VMEM((sides, wins, 4 * EDGE, width), BF16),
            pltpu.VMEM((sides, wins, 4 * EDGE, width), BF16),
            pltpu.VMEM((wins * TOK, width), BF16),
            pltpu.VMEM((wins * TOK, width), BF16),
            pltpu.VMEM((rows, long), F32),
            pltpu.VMEM((heads * WIN_LEVEL * block, 256), F32),
            pltpu.VMEM((tiles, TOK * wins, 128), F32),
            pltpu.VMEM((tiles, TOK * wins, 128), F32),
            pltpu.VMEM((4, wins * TOK, inner), BF16),
            pltpu.VMEM((3, inner, groups * 128), BF16),
            pltpu.VMEM((wins, groups, packed, 128), BF16),
            pltpu.VMEM((wins, groups - 1, packed, 128), BF16),
            pltpu.VMEM((sides, wins, 2 * EDGE, inner), BF16),
            pltpu.VMEM((2, 2 * inner, width), BF16),
            pltpu.VMEM((2 * inner, width), BF16),
            pltpu.VMEM((steps + 1, 2, inner, width), BF16),
            pltpu.VMEM((steps, 2, inner, width), BF16),
            pltpu.VMEM((lon_steps + 1, rows, long), BF16),
            pltpu.VMEM((lon_steps, rows, long), BF16),
            dma((5,)),
            dma((2, wins * sides)),
            dma((2, wins * (groups - 1))),
            dma((2, wins * sides)),
            dma((2, 2 * steps + 3)),
            dma((2, lon_steps + lats - 1)),
        ],
        compiler_params=pltpu.CompilerParams(
            collective_id=0, has_side_effects=True, vmem_limit_bytes=54 * 1024 * 1024
        ),
        cost_estimate=pl.CostEstimate(flops=10**9, bytes_accessed=10**7, transcendentals=10**6),
    )(shift, types, x, g, aw, ow, table)


def finish_kernel(lons, shift_ref, own_ref, edge_ref, w_ref, bias_ref,
                  feature_ref, aw_ref, ow_ref, table_ref, wide, edges):
    shift = shift_ref[0]
    early = shift <= HALF
    wins = own_ref.shape[0]
    chunk = own_ref.shape[2]
    levels = wins * WIN_LEVEL
    sides = edge_ref.shape[0]
    for w in range(wins):
        full = own_ref[w].astype(F32)
        if sides == 1:
            rim = edge_ref[0, w].astype(F32)
        else:
            rim = jnp.where(early, edge_ref[0, w].astype(F32), edge_ref[1, w].astype(F32))
        for z in range(WIN_LEVEL):
            level = WIN_LEVEL * w + z
            wide[pl.ds(level, SIDE, stride=levels), :chunk] = full[z * SIDE:(z + 1) * SIDE]
            edges[pl.ds(level, EDGE, stride=levels), :chunk] = rim[z * EDGE:(z + 1) * EDGE]
    run = WIN_LAT * levels
    for c in range(WIN_LON):
        here = lax.rem(c + WIN_LON - shift, WIN_LON)
        there = jnp.where(early, jnp.maximum(HALF + c - shift, 0), jnp.maximum(c - shift, 0))
        there = jnp.minimum(there, HALF - 1)
        flag = jnp.where(early, (c >= shift).astype(F32), (c < shift).astype(F32))
        near = wide[pl.ds(pl.multiple_of(here * run, 8), run), :]
        far = edges[pl.ds(pl.multiple_of(there * run, 8), run), :]
        mixed = near * flag + far * (1.0 - flag)
        feature_ref[:, c] = mixed.reshape(WIN_LAT, levels, 128)[:, :, :chunk].astype(BF16)
    inner = aw_ref.shape[1]
    flat = w_ref[...].reshape(4 * inner, w_ref.shape[2])
    for c in range(3):
        aw_ref[c] = flat[c * inner:(c + 1) * inner].astype(F32)
    ow_ref[...] = flat[3 * inner:].astype(F32)

    heads, types, total = table_ref.shape
    lats, rows, long = bias_ref.shape
    lines = bias_ref[...].reshape(lats * rows, long)
    kinds = lines[:, total:total + 1].astype(F32)
    held = lax.broadcasted_iota(jnp.int32, (lats * rows, types), 0) % rows // wins
    kind = lax.broadcasted_iota(jnp.int32, (lats * rows, types), 1).astype(F32)
    for h in range(heads):
        pick = jnp.where((kinds == kind) & (held == h), 1.0, 0.0).astype(BF16)
        table_ref[h] = dot(pick, lines, TN)[:, :total]


def finish(own, edge, all_w, all_bias, shift, types, heads, rel_total):
    wins, _, chunk = own.shape
    inner = all_w.shape[1] // 2
    levels = wins * WIN_LEVEL
    vmem = pl.BlockSpec(memory_space=pltpu.VMEM)
    return pl.pallas_call(
        functools.partial(finish_kernel, lax.axis_size("lon")),
        out_shape=(
            jax.ShapeDtypeStruct((WIN_LAT, WIN_LON, levels, chunk), BF16),
            jax.ShapeDtypeStruct((3, inner, all_w.shape[2]), F32),
            jax.ShapeDtypeStruct((inner, all_w.shape[2]), F32),
            jax.ShapeDtypeStruct((heads, types, rel_total), F32),
        ),
        in_specs=[pl.BlockSpec(memory_space=pltpu.SMEM)] + [vmem] * 4,
        out_specs=(vmem,) * 4,
        scratch_shapes=[
            pltpu.VMEM((SIDE * levels, 128), F32),
            pltpu.VMEM((EDGE * levels, 128), F32),
        ],
        compiler_params=pltpu.CompilerParams(vmem_limit_bytes=20 * 1024 * 1024),
    )(shift, own, edge, all_w, all_bias)


def per_device(features, attend_weight, output_weight, bias_table, bias_type, window_shift, grad_out):
    x, g = (v.transpose(1, 2, 0, 3) for v in (features, grad_out))
    aw = attend_weight.transpose(0, 2, 1)
    table = bias_table.transpose(1, 0, 2)
    gathered = block_backward(x, g, aw, output_weight, table, bias_type.T, window_shift)
    types, heads, rel_total = bias_table.shape
    feature_grad, attend_grad, output_grad, bias_grad = finish(*gathered, window_shift, types, heads, rel_total)
    return (
        feature_grad.transpose(2, 0, 1, 3),
        attend_grad.transpose(0, 2, 1),
        output_grad,
        bias_grad.transpose(1, 0, 2),
    )


def solution(mesh):
    placed = (
        P(None, "lat", "lon", None),
        P(None, None, "head"),
        P("head", None),
        P(None, "head", None),
        P(None, "lat"),
        P(),
        P(None, "lat", "lon", None),
    )
    return jax.shard_map(
        per_device,
        mesh=mesh,
        in_specs=placed,
        out_specs=(
            P(None, "lat", "lon", "head"),
            P(None, None, "head"),
            P("head", None),
            P(None, "head", None),
        ),
        check_vma=False,
    )
```

time: 53.1 us -> 38 us (0.72)
  local copies, waits for them, and re-layouts: 10.4 us -> 0 us
  starting transfers between devices: 2.97 us -> 0 us
  other arithmetic: 0.85 us -> 0 us
  Pallas kernels: 37.1 us -> 36.5 us
    unnamed x25 -> x0, local copies, waits for them, and re-layouts: 7.82 us -> none
    ppermute x1 -> x0, starting transfers between devices: 2.97 us -> none  [from_behind(): return lax.ppermute(x, axis, [(i, (i + by) % count) for i in range(count)])]
    another operation x1 -> x0, local copies, waits for them, and re-layouts: 1.5 us -> none  [per_device(): jnp.stack([x[:, HALF:] for x in stored])]
    transpose x1 -> x0, local copies, waits for them, and re-layouts: 1.1 us -> none  [per_device(): x.transpose(0, 3, 1, 2, 4).reshape(2, levels * lat_rows, HALF, width)]
    select_n x1 -> x0, other arithmetic: 0.85 us -> none  [swap_columns(): got = from_behind(jnp.where(shift <= HALF, low, high), 'lon', 1)]
    pallas_call x4 -> x2, Pallas kernels: 37.1 us -> 36.5 us  [the longest x1 34.2 us: block_backward(): pl.pallas_call(functools.partial(block_kernel, heads), out_shape=(pltpu.V...]
  transfers between devices with their start and end apart: 1 -> 0, of which waited for: 0 -> 0; matrix products, arithmetic and copies ran while one was open for 10% -> 0% of each run, Pallas kernels for 7% -> 0%
where the time goes in v1:
time: 38 us; the launch traced here: 37.8 us
  Pallas kernels  36.5 us (96%)
  between operations  1.29 us (3%)
    pallas_call x1, Pallas kernels, block_backward(): pl.pallas_call(functools.partial(block_kernel, heads), out_shape=(pltpu.V...  34.2 us
    pallas_call x1, Pallas kernels, finish(): pl.pallas_call(functools.partial(finish_kernel, lax.axis_size('lon')), ou...  2.36 us

profile of v1, /device:TPU:0, one launch (start us, length us, event | category | flops | bytes accessed | tf_op | source)
XLA Modules:
  0.0 37.8 jit_solution(407020355021443074)
XLA Ops:
  1.3 34.2 %shard_map.102 = (bf16[4,144,96]{2,1,0:T(8,128)(2,1)S(1)}, bf16[1,4,72,96]{3,2,1,0:T(8,128)(2,1)S(1)}, bf16[2,192,384]{2,1,0:T(8,128)(2,1)S(1)}, bf16[4,16,3328]{2,1,0:T(8,128)(2,1)S(1)}) custom-call(s32[1]{0:T(128)S(6)} %copy.11.shift_ref, s32[1,4]{1,0:T(1,128)} %bitcast.12, bf16[6,12,8,384]{3,2,1,0:T(8,128)(2,1)} %bitcast.9, ...), custom_call_target="tpu_custom_call" | custom-call | flops 1000000000 | bytes 10000000 | tf_op jit(solution)/shard_map/pallas_call | solution.py:449
  35.4 2.4 %shard_map.103 = (bf16[6,12,8,96]{3,2,1,0:T(8,128)(2,1)}, f32[3,96,384]{2,1,0:T(8,128)}, f32[96,384]{1,0:T(8,128)}, f32[3,64,3312]{2,1,0:T(8,128)}) custom-call(s32[1]{0:T(128)S(6)} %copy.11.shift_ref, bf16[4,144,96]{2,1,0:T(8,128)(2,1)S(1)} %get-tuple-element.12.own_ref, bf16[1,4,72,96]{3,2,1,0:T(8,128)(2,1)S(1)} %get-tuple-element.13.edge_ref, ...), custom_call_target="tpu_custom_call" | custom-call | tf_op jit(solution)/shard_map/pallas_call | solution.py:550

commit v2 on v1

--- a/solution.py
+++ b/solution.py
@@ -50,6 +50,15 @@
     return jnp.where(place == out, 1.0, 0.0).astype(BF16)
 
 
+def back_permutation(lanes):
+    row = lax.broadcasted_iota(jnp.int32, (256, lanes), 0)
+    out = lax.broadcasted_iota(jnp.int32, (256, lanes), 1)
+    at = row % 128
+    d = at // WIN_LAT + jnp.where(row >= 128, WIN_LON, 0)
+    hit = (at % WIN_LAT * PART + d == out) & (at < SIDE) & (d < SPAN)
+    return jnp.where(hit, 1.0, 0.0).astype(BF16)
+
+
 def lane_lon(lanes):
     return lax.broadcasted_iota(jnp.int32, (1, lanes), 1) % SIDE // WIN_LAT
 
@@ -58,7 +67,7 @@
                  own_ref, edge_ref, all_w_ref, all_bias_ref,
                  x_own, g_own, aw, ow, table, halo_f, own_f, halo_out, halo_in, xs, gs,
                  line, parts, bias, gbias, gp, aw_split, piece_out, piece_in, edge_out,
-                 w_core, w_core_in, w_cur, w_in, bias_cur, bias_in,
+                 w_core, w_core_in, w_cur, w_in, bias_cur, bias_in, folds, spots_f, rows_f,
                  local, halo_sem, piece_sem, edge_sem, w_sem, bias_sem):
     lons, lats, groups = (lax.axis_size(name) for name in ("lon", "lat", "head"))
     lon, lat, head = (lax.axis_index(name) for name in ("lon", "lat", "head"))
@@ -288,9 +297,92 @@
             copy.start()
             edge_copies.append(copy)
 
+    strip_b = bias_cur.shape[2]
+    back = back_permutation(rows_f.shape[0] * 128)
+    folds[...] = jnp.zeros_like(folds)
+    count_b = [0]
+    bias_copies = []
+
+    def post_b(src, dst, device):
+        copy = remote(src, dst, bias_sem, count_b[0], device)
+        count_b[0] += 1
+        copy.start()
+        bias_copies.append(copy)
+        return copy
+
+    def bias_line(w):
+        for z in range(WIN_LEVEL):
+            low = jnp.zeros((WIN_LAT, lanes), F32)
+            high = jnp.zeros((WIN_LAT, lanes), F32)
+            for b in range(WIN_LON):
+                rows = pl.ds((z * WIN_LON + b) * half + w, WIN_LAT, stride=wins)
+                got = jnp.concatenate([gbias[t, rows, :] for t in range(tiles)], axis=1)
+                right = WIN_LAT * (WIN_LON - 1 - b)
+                low = low + pltpu.roll(jnp.where(place <= b, got, 0.0), right, 1)
+                high = high + pltpu.roll(jnp.where(place > b, got, 0.0), lanes - WIN_LAT * (b + 1), 1)
+            for g in range(segs):
+                r = (g * WIN_LEVEL + z) * 8
+                folds[r:r + WIN_LAT, :SIDE] = low[:, g * SIDE:(g + 1) * SIDE]
+                folds[r:r + WIN_LAT, 128:128 + SIDE] = high[:, g * SIDE:(g + 1) * SIDE]
+        spread_out = dot(folds[...].astype(BF16), back, NN)
+        count = segs * WIN_LEVEL
+        for t in range(spots_f.shape[0]):
+            spots_f[t] = spread_out[:, t * 128:(t + 1) * 128]
+        sums = jnp.zeros((count, spots_f.shape[0] * 128), F32)
+        for a in range(WIN_LAT):
+            rows = pl.ds(a, count, stride=8)
+            got = jnp.concatenate([spots_f[t, rows, :] for t in range(spots_f.shape[0])], axis=1)
+            sums = sums + (pltpu.roll(got, a * SPAN, 1) if a else got)
+        for t in range(rows_f.shape[0]):
+            rows_f[t, :count, :] = sums[:, t * 128:(t + 1) * 128]
+        quarters = WIN_LEVEL * WIN_LEVEL
+        run = WIN_LAT * PART
+        found = []
+        for q in range(quarters):
+            rows = pl.ds(q, heads, stride=quarters)
+            found.append(jnp.concatenate([rows_f[t, rows, :] for t in range(rows_f.shape[0])], axis=1)[:, :run])
+        found.append(jnp.zeros((heads, 2 * strip_b - quarters * run), F32))
+        full = jnp.concatenate(found, axis=1)
+        both = [full[:, :strip_b], full[:, strip_b:], jnp.zeros((8 - 2 * heads, strip_b), F32)]
+        bias_cur[0, w * 8:(w + 1) * 8, :] = jnp.concatenate(both, axis=0).astype(BF16)
+        return post_b(bias_cur.at[0, pl.ds(w * 8, 8)], bias_in.at[0, pl.ds(w * 8, 8)], mates[0])
+
+    lon_steps = len(lon_bits)
+
+    def bias_total(first, last, flights):
+        rows, span = slice(first * 8, last * 8), pl.ds(first * 8, (last - first) * 8)
+        for k in range(lon_steps):
+            for copy in flights:
+                copy.wait_recv()
+            fresh = bias_cur[k, rows, :].astype(F32) + bias_in[k, rows, :].astype(F32)
+            if k + 1 == lon_steps:
+                row = lax.broadcasted_iota(jnp.int32, fresh.shape, 0)
+                for w in range(first, last):
+                    fresh = jnp.where(row == (w - first) * 8 + 2 * heads, type_ref[0, w].astype(F32), fresh)
+            bias_cur[k + 1, rows, :] = fresh.astype(BF16)
+            if k + 1 < lon_steps:
+                flights = [post_b(bias_cur.at[k + 1, span], bias_in.at[k + 1, span], mates[k + 1])]
+        all_bias_ref[pl.ds(lat, 1), rows, :] = bias_cur[lon_steps, rows, :][None]
+        return span
+
+    gather_order = list(reversed(list(zip(lat_bits, rows_up))))
+
+    def bias_gather(step, span, have, flights):
+        for copy in flights:
+            copy.wait_recv()
+        bit, device = gather_order[step]
+        out = []
+        for slot in have:
+            src = bias_cur.at[lon_steps, span] if slot is lat else all_bias_ref.at[slot, span]
+            out.append(post_b(src, all_bias_ref.at[slot, span], device))
+        return have + [flip(slot, bit) for slot in have], out
+
+    lines = []
     for w in range(wins):
         window(w)
         send_pieces(w)
+        if w < wins - 1:
+            lines.append(bias_line(w))
         if w >= 2:
             sum_pieces(w - 2)
 
@@ -314,19 +406,9 @@
     core_mate = rows_up[0]
     swap = post_w(w_core.at[1 - keep], w_core_in, core_mate)
 
-    low_sum = jnp.zeros((block, lanes), F32)
-    high_sum = jnp.zeros((block, lanes), F32)
-    for b in range(WIN_LON):
-        got = jnp.concatenate(
-            [
-                jnp.concatenate([gbias[t, (z * WIN_LON + b) * half:(z * WIN_LON + b + 1) * half, :] for t in range(tiles)], axis=1)
-                for z in range(WIN_LEVEL)
-            ],
-            axis=0,
-        )
-        right = WIN_LAT * (WIN_LON - 1 - b)
-        low_sum = low_sum + pltpu.roll(jnp.where(place <= b, got, 0.0), right, 1)
-        high_sum = high_sum + pltpu.roll(jnp.where(place > b, got, 0.0), lanes - WIN_LAT * (b + 1), 1)
+    early_span = bias_total(0, wins - 1, lines)
+    early_have, early_out = bias_gather(0, early_span, [lat], [])
+    last_line = bias_line(wins - 1)
 
     swap.wait_recv()
     sub = part_w // 2
@@ -341,37 +423,7 @@
         w_cur[0, j] = (w_core[keep, part, :].astype(F32) + w_core_in[part, :].astype(F32)).astype(BF16)
         flying[j] = post_w(w_cur.at[0, j], w_in.at[0, j], orders[j][0][1])
 
-    gap = jnp.zeros((block, 128 - SIDE), F32)
-    sums = jnp.concatenate(
-        [
-            jnp.concatenate(
-                [low_sum[:, s * SIDE:(s + 1) * SIDE], gap, high_sum[:, s * SIDE:(s + 1) * SIDE], gap], axis=1
-            )
-            for s in range(segs)
-        ],
-        axis=0,
-    ).astype(BF16)
-    parts[:, :PART] = dot(sums, perm, NT)
-    for k, h, r, c in spots:
-        line[h * wins:(h + 1) * wins, k * SPAN:(k + 1) * SPAN] = parts[r:r + wins, c:c + SPAN]
-    used = lax.broadcasted_iota(jnp.int32, line.shape, 0) < heads * wins
-    inside = lax.broadcasted_iota(jnp.int32, line.shape, 1) < table.shape[2]
-    bias_cur[0] = jnp.where(used & inside, line[...], 0.0).astype(BF16)
-    count_b = [0]
-    bias_copies = []
-
-    def post_b(src, dst, device):
-        copy = remote(src, dst, bias_sem, count_b[0], device)
-        count_b[0] += 1
-        copy.start()
-        bias_copies.append(copy)
-        return copy
-
-    bias_step = post_b(bias_cur.at[0], bias_in.at[0], mates[0])
-
-    for w in range(max(wins - 2, 0), wins):
-        if w == wins - 1:
-            break
+    for w in range(max(wins - 2, 0), wins - 1):
         sum_pieces(w)
 
     def w_step(k):
@@ -382,38 +434,16 @@
             if k + 1 < steps:
                 flying[j] = post_w(w_cur.at[k + 1, j], w_in.at[k + 1, j], orders[j][k + 1][1])
 
-    def bias_sum(k):
-        bias_copies[k].wait_recv()
-        fresh = bias_cur[k].astype(F32) + bias_in[k].astype(F32)
-        if k + 1 < len(lon_bits):
-            bias_cur[k + 1] = fresh.astype(BF16)
-            post_b(bias_cur.at[k + 1], bias_in.at[k + 1], mates[k + 1])
-        else:
-            kind_row = lax.broadcasted_iota(jnp.int32, line.shape, 0) % wins
-            kind = jnp.zeros(line.shape, F32)
-            for w in range(wins):
-                kind = jnp.where(kind_row == w, type_ref[0, w].astype(F32), kind)
-            bias_cur[k + 1] = jnp.where(inside, fresh, kind).astype(BF16)
-            all_bias_ref[pl.ds(lat, 1)] = bias_cur[k + 1][None]
-
-    for k in range(len(lon_bits)):
-        bias_sum(k)
-    final = bias_cur.at[len(lon_bits)]
-    spread_copies = []
-    have = [lat]
-    order = list(reversed(list(zip(lat_bits, rows_up))))
-    for i, (b, device) in enumerate(order):
-        for slot in have:
-            src = final if slot is lat else all_bias_ref.at[slot]
-            spread_copies.append(post_b(src, all_bias_ref.at[slot], device))
-        have = have + [flip(slot, b) for slot in have]
+    late_have, late_out = [lat], []
+    for i in range(len(gather_order)):
+        if i + 1 < len(gather_order):
+            early_have, early_out = bias_gather(i + 1, early_span, early_have, early_out)
+        if i == 0:
+            late_span = bias_total(wins - 1, wins, [last_line])
+        late_have, late_out = bias_gather(i, late_span, late_have, late_out)
         if i == 0:
             w_step(0)
             sum_pieces(wins - 1)
-        if i + 1 < len(order):
-            for copy in spread_copies:
-                copy.wait_recv()
-            spread_copies = []
     for k in range(1, steps):
         w_step(k)
     both_w = [
@@ -421,7 +451,7 @@
     ]
     for j in range(2):
         all_w_ref[pl.ds(keep, 1), j * sub:(j + 1) * sub, :] = w_cur[steps, j][None]
-    for copy in both_w + spread_copies + edge_copies:
+    for copy in both_w + early_out + late_out + edge_copies:
         copy.wait_recv()
     for copy in sent + piece_copies + edge_copies + w_copies + bias_copies:
         copy.wait_send()
@@ -442,6 +472,8 @@
     lon_steps = len(bits_of(lons))
     steps = lon_steps + len(bits_of(lats)) - 1
     packed = up(MAIN, 16)
+    strip = up(rel_total, 256) // 2
+    quads = heads * WIN_LEVEL * WIN_LEVEL
     vmem = pl.BlockSpec(memory_space=pltpu.VMEM)
     smem = pl.BlockSpec(memory_space=pltpu.SMEM)
     hbm = pl.BlockSpec(memory_space=pltpu.HBM)
@@ -452,7 +484,7 @@
             pltpu.VMEM((wins, TOK, inner), BF16),
             pltpu.VMEM((sides, wins, 2 * EDGE, inner), BF16),
             pltpu.VMEM((2, 2 * inner, width), BF16),
-            pltpu.VMEM((lats, rows, long), BF16),
+            pltpu.VMEM((lats, wins * 8, strip), BF16),
         ),
         in_specs=[smem, smem] + [hbm] * 5,
         out_specs=(vmem,) * 4,
@@ -481,14 +513,17 @@
             pltpu.VMEM((2 * inner, width), BF16),
             pltpu.VMEM((steps + 1, 2, inner, width), BF16),
             pltpu.VMEM((steps, 2, inner, width), BF16),
-            pltpu.VMEM((lon_steps + 1, rows, long), BF16),
-            pltpu.VMEM((lon_steps, rows, long), BF16),
+            pltpu.VMEM((lon_steps + 1, wins * 8, strip), BF16),
+            pltpu.VMEM((lon_steps, wins * 8, strip), BF16),
+            pltpu.VMEM((quads * 8, 256), F32),
+            pltpu.VMEM((up(WIN_LAT * PART, 128) // 128, quads * 8, 128), F32),
+            pltpu.VMEM((up(WIN_LAT * PART, 128) // 128, up(quads, 8), 128), F32),
             dma((5,)),
             dma((2, wins * sides)),
             dma((2, wins * (groups - 1))),
             dma((2, wins * sides)),
             dma((2, 2 * steps + 3)),
-            dma((2, lon_steps + lats - 1)),
+            dma((2, wins + 2 * (lon_steps - 1) + 2 * (lats - 1))),
         ],
         compiler_params=pltpu.CompilerParams(
             collective_id=0, has_side_effects=True, vmem_limit_bytes=54 * 1024 * 1024
@@ -497,14 +532,45 @@
     )(shift, types, x, g, aw, ow, table)
 
 
-def finish_kernel(lons, shift_ref, own_ref, edge_ref, w_ref, bias_ref,
-                  feature_ref, aw_ref, ow_ref, table_ref, wide, edges):
+def finish_kernel(shift_ref, own_ref, edge_ref, w_ref, bias_ref,
+                  feature_out, aw_out, ow_out, table_out,
+                  feature, aw, ow, table, wide, edges, sems):
     shift = shift_ref[0]
     early = shift <= HALF
     wins = own_ref.shape[0]
     chunk = own_ref.shape[2]
     levels = wins * WIN_LEVEL
     sides = edge_ref.shape[0]
+    heads, types, total = table.shape
+    lats, _, strip = bias_ref.shape
+    copies = []
+
+    def put(src, dst):
+        copy = pltpu.make_async_copy(src, dst, sems.at[len(copies)])
+        copy.start()
+        copies.append(copy)
+
+    count = lats * wins
+    lines = bias_ref[...].reshape(count * 8, strip)
+    kinds = lines[:, :128].astype(F32).reshape(count, 8, 128)[:, 2 * heads:2 * heads + 1, :types]
+    kind = lax.broadcasted_iota(jnp.int32, (count, 8, types), 2).astype(F32)
+    row = lax.broadcasted_iota(jnp.int32, (count, 8, types), 1)
+    same = kinds == kind
+    for h in range(heads):
+        for p in range(2):
+            pick = jnp.where(same & (row == p * heads + h), 1.0, 0.0).reshape(count * 8, types).astype(BF16)
+            stop = min(total, (p + 1) * strip)
+            table[h, :, p * strip:stop] = dot(pick, lines, TN)[:, :stop - p * strip]
+        put(table.at[h], table_out.at[h])
+
+    inner = aw.shape[1]
+    flat = w_ref[...].reshape(4 * inner, w_ref.shape[2])
+    for c in range(3):
+        aw[c] = flat[c * inner:(c + 1) * inner].astype(F32)
+    ow[...] = flat[3 * inner:].astype(F32)
+    put(aw, aw_out)
+    put(ow, ow_out)
+
     for w in range(wins):
         full = own_ref[w].astype(F32)
         if sides == 1:
@@ -520,26 +586,14 @@
         here = lax.rem(c + WIN_LON - shift, WIN_LON)
         there = jnp.where(early, jnp.maximum(HALF + c - shift, 0), jnp.maximum(c - shift, 0))
         there = jnp.minimum(there, HALF - 1)
-        flag = jnp.where(early, (c >= shift).astype(F32), (c < shift).astype(F32))
+        local = jnp.where(early, (c >= shift).astype(F32), (c < shift).astype(F32)) > 0.5
         near = wide[pl.ds(pl.multiple_of(here * run, 8), run), :]
         far = edges[pl.ds(pl.multiple_of(there * run, 8), run), :]
-        mixed = near * flag + far * (1.0 - flag)
-        feature_ref[:, c] = mixed.reshape(WIN_LAT, levels, 128)[:, :, :chunk].astype(BF16)
-    inner = aw_ref.shape[1]
-    flat = w_ref[...].reshape(4 * inner, w_ref.shape[2])
-    for c in range(3):
-        aw_ref[c] = flat[c * inner:(c + 1) * inner].astype(F32)
-    ow_ref[...] = flat[3 * inner:].astype(F32)
-
-    heads, types, total = table_ref.shape
-    lats, rows, long = bias_ref.shape
-    lines = bias_ref[...].reshape(lats * rows, long)
-    kinds = lines[:, total:total + 1].astype(F32)
-    held = lax.broadcasted_iota(jnp.int32, (lats * rows, types), 0) % rows // wins
-    kind = lax.broadcasted_iota(jnp.int32, (lats * rows, types), 1).astype(F32)
-    for h in range(heads):
-        pick = jnp.where((kinds == kind) & (held == h), 1.0, 0.0).astype(BF16)
-        table_ref[h] = dot(pick, lines, TN)[:, :total]
+        mixed = jnp.where(local, near, far)
+        feature[:, c] = mixed.reshape(WIN_LAT, levels, 128)[:, :, :chunk].astype(BF16)
+    put(feature, feature_out)
+    for copy in copies:
+        copy.wait()
 
 
 def finish(own, edge, all_w, all_bias, shift, types, heads, rel_total):
@@ -547,19 +601,21 @@
     inner = all_w.shape[1] // 2
     levels = wins * WIN_LEVEL
     vmem = pl.BlockSpec(memory_space=pltpu.VMEM)
+    outs = (
+        ((WIN_LAT, WIN_LON, levels, chunk), BF16),
+        ((3, inner, all_w.shape[2]), F32),
+        ((inner, all_w.shape[2]), F32),
+        ((heads, types, rel_total), F32),
+    )
     return pl.pallas_call(
-        functools.partial(finish_kernel, lax.axis_size("lon")),
-        out_shape=(
-            jax.ShapeDtypeStruct((WIN_LAT, WIN_LON, levels, chunk), BF16),
-            jax.ShapeDtypeStruct((3, inner, all_w.shape[2]), F32),
-            jax.ShapeDtypeStruct((inner, all_w.shape[2]), F32),
-            jax.ShapeDtypeStruct((heads, types, rel_total), F32),
-        ),
+        finish_kernel,
+        out_shape=tuple(jax.ShapeDtypeStruct(*out) for out in outs),
         in_specs=[pl.BlockSpec(memory_space=pltpu.SMEM)] + [vmem] * 4,
-        out_specs=(vmem,) * 4,
-        scratch_shapes=[
+        out_specs=(pl.BlockSpec(memory_space=pl.ANY),) * 4,
+        scratch_shapes=[pltpu.VMEM(*out) for out in outs] + [
             pltpu.VMEM((SIDE * levels, 128), F32),
             pltpu.VMEM((EDGE * levels, 128), F32),
+            pltpu.SemaphoreType.DMA((heads + 3,)),
         ],
         compiler_params=pltpu.CompilerParams(vmem_limit_bytes=20 * 1024 * 1024),
     )(shift, own, edge, all_w, all_bias)

time: 38 us -> 34.9 us (0.918)
  Pallas kernels: 36.5 us -> 33.4 us
    pallas_call x1, Pallas kernels: 34.2 us -> 31.3 us  [block_backward(): pl.pallas_call(functools.partial(block_kernel, heads), out_shape=(pltpu.V...]
where the time goes in v2:
time: 34.9 us; the launch traced here: 34.7 us
  Pallas kernels  33.4 us (96%)
  between operations  1.29 us (4%)
    pallas_call x1, Pallas kernels, block_backward(): pl.pallas_call(functools.partial(block_kernel, heads), out_shape=(pltpu.V...  31.3 us
    pallas_call x1, Pallas kernels, finish(): pl.pallas_call(finish_kernel, out_shape=tuple((jax.ShapeDtypeStruct(*out)...  2.11 us

profile of v2, /device:TPU:0, one launch (start us, length us, event | category | flops | bytes accessed | tf_op | source)
XLA Modules:
  0.0 34.7 jit_solution(11490531529871494720)
XLA Ops:
  1.3 31.3 %shard_map.102 = (bf16[4,144,96]{2,1,0:T(8,128)(2,1)S(1)}, bf16[1,4,72,96]{3,2,1,0:T(8,128)(2,1)S(1)}, bf16[2,192,384]{2,1,0:T(8,128)(2,1)S(1)}, bf16[4,32,1664]{2,1,0:T(8,128)(2,1)S(1)}) custom-call(s32[1]{0:T(128)S(6)} %copy.11.shift_ref, s32[1,4]{1,0:T(1,128)} %bitcast.12, bf16[6,12,8,384]{3,2,1,0:T(8,128)(2,1)} %bitcast.9, ...), custom_call_target="tpu_custom_call" | custom-call | flops 1000000000 | bytes 10000000 | tf_op jit(solution)/shard_map/pallas_call | solution.py:481
  32.6 2.1 %shard_map.103 = (bf16[6,12,8,96]{3,2,1,0:T(8,128)(2,1)}, f32[3,96,384]{2,1,0:T(8,128)}, f32[96,384]{1,0:T(8,128)}, f32[3,64,3312]{2,1,0:T(8,128)}) custom-call(s32[1]{0:T(128)S(6)} %copy.11.shift_ref, bf16[4,144,96]{2,1,0:T(8,128)(2,1)S(1)} %get-tuple-element.12.own_ref, bf16[1,4,72,96]{3,2,1,0:T(8,128)(2,1)S(1)} %get-tuple-element.13.edge_ref, ...), custom_call_target="tpu_custom_call" | custom-call | tf_op jit(solution)/shard_map/pallas_call | solution.py:610

commit v3 on v2

--- a/solution.py
+++ b/solution.py
@@ -63,16 +63,24 @@
     return lax.broadcasted_iota(jnp.int32, (1, lanes), 1) % SIDE // WIN_LAT
 
 
-def block_kernel(heads, shift_ref, type_ref, x_hbm, g_hbm, aw_hbm, ow_hbm, table_hbm,
+def tail_order(wins, steps, gathers):
+    tasks = [("piece", w) for w in range(2, wins - 1)]
+    tasks += [("w", 0), ("sum", 0), ("late", 0)] + [("early", i) for i in range(1, gathers)]
+    tasks += [("piece", wins - 1)] + [("w", k) for k in range(1, steps)] + [("late", i) for i in range(1, gathers)]
+    return tasks
+
+
+def block_kernel(heads, reach, shift_ref, type_ref, x_hbm, g_hbm, aw_hbm, ow_hbm, table_hbm,
                  own_ref, edge_ref, all_w_ref, all_bias_ref,
                  x_own, g_own, aw, ow, table, halo_f, own_f, halo_out, halo_in, xs, gs,
                  line, parts, bias, gbias, gp, aw_split, piece_out, piece_in, edge_out,
-                 w_core, w_core_in, w_cur, w_in, bias_cur, bias_in, folds, spots_f, rows_f,
+                 w_core, w_core_in, w_cur, w_in, bias_cur, bias_in, w_acc, folds, spots_f, rows_f,
                  local, halo_sem, piece_sem, edge_sem, w_sem, bias_sem):
     lons, lats, groups = (lax.axis_size(name) for name in ("lon", "lat", "head"))
     lon, lat, head = (lax.axis_index(name) for name in ("lon", "lat", "head"))
     shift = shift_ref[0]
     early = shift <= HALF
+    rim = reach * WIN_LAT
     cols, levels, width = x_own.shape[1:]
     wins = levels // WIN_LEVEL
     inner = aw.shape[1]
@@ -124,8 +132,8 @@
     sent = []
     for n in range(len(sides)):
         for i, src in enumerate((x_own, g_own)):
-            for b in range(HALF):
-                low = jnp.maximum(shift + b - HALF, 0)
+            for b in range(reach):
+                low = jnp.maximum(shift + b - reach, 0)
                 high = jnp.minimum(shift + b, cols - 1)
                 if lons <= 2:
                     col = jnp.where(early, low, high)
@@ -134,9 +142,8 @@
                 for a in range(WIN_LAT):
                     put(halo_f, i, b * WIN_LAT + a, src[a, col])
         for w in range(wins):
-            for i in range(2):
-                rows = [take(halo_f, i, WIN_LEVEL * w + z, EDGE) for z in range(WIN_LEVEL)]
-                halo_out[n, w, i * 2 * EDGE:(i + 1) * 2 * EDGE, :] = jnp.concatenate(rows, axis=0).astype(BF16)
+            rows = [take(halo_f, i, WIN_LEVEL * w + z, rim) for i in range(2) for z in range(WIN_LEVEL)]
+            halo_out[n, w] = jnp.concatenate(rows, axis=0).astype(BF16)
     pl.semaphore_wait(barrier, len(greet))
     for w in range(wins):
         for n, device in enumerate(sides):
@@ -194,12 +201,11 @@
 
     loads[3].wait()
     loads[4].wait()
+    gp[...] = jnp.zeros_like(gp)
+    aw_split[...] = jnp.zeros_like(aw_split)
     for c in range(3):
         for g in range(groups):
-            chunk = aw[c, :, g * inner:(g + 1) * inner]
-            aw_split[c, :, g * 128:(g + 1) * 128] = jnp.concatenate(
-                [chunk, jnp.zeros((inner, 128 - inner), BF16)], axis=1
-            )
+            aw_split[c * 128:c * 128 + inner, g * 128:g * 128 + inner] = aw[c, :, g * inner:(g + 1) * inner]
 
     key_lon = lax.broadcasted_iota(jnp.int32, (TOK, 1), 0) % SIDE // WIN_LAT
     mine = jnp.where(early, (key_lon + shift < WIN_LON).astype(F32), (key_lon + shift >= WIN_LON).astype(F32)) > 0.5
@@ -227,12 +233,17 @@
         span = slice(w * TOK, (w + 1) * TOK)
         for n in range(len(sides)):
             sent[w * len(sides) + n].wait_recv()
+        arrived = [halo_in[n, w].astype(F32) for n in range(len(sides))]
         for i, dst in enumerate((xs, gs)):
             kept = [take(own_f, i, WIN_LEVEL * w + z, SIDE) for z in range(WIN_LEVEL)]
             kept = jnp.concatenate(kept, axis=0)
-            near = [halo_in[n, w, i * 2 * EDGE:(i + 1) * 2 * EDGE, :].astype(F32) for n in range(len(sides))]
-            first, last = (near[0], near[0]) if lons <= 2 else (near[0], near[1])
-            filled = jnp.concatenate([first[:EDGE], last[:EDGE], first[EDGE:], last[EDGE:]], axis=0)
+            near = [got[i * 2 * rim:(i + 1) * 2 * rim] for got in arrived]
+            first, last = near[0], near[-1]
+            filled = []
+            for z in range(WIN_LEVEL):
+                part, start = slice(z * rim, (z + 1) * rim), z * SIDE
+                filled += [first[part], kept[start + rim:start + SIDE - rim], last[part]]
+            filled = jnp.concatenate([f for f in filled if f.shape[0]], axis=0)
             dst[span, :] = jnp.where(mine, kept, filled).astype(BF16)
         tokens, grads = xs[span, :], gs[span, :]
         queries = expanded(dot(aw[0], tokens, NT))
@@ -251,14 +262,14 @@
         for t in range(tiles):
             gbias[t, rows, :] = slopes[:, t * 128:(t + 1) * 128]
         slopes_half = slopes.astype(BF16)
-        gp[0, span, :] = (folded(dot(slopes_half, keys, TN)) * scaling).astype(BF16)
-        gp[1, span, :] = (dot(slopes_half, queries, NT) * scaling).astype(BF16)
-        gp[2, span, :] = dot(soft_half, gates, NT).astype(BF16)
-        gp[3, span, :] = folded(dot(soft_half, values, TN)).astype(BF16)
+        gp[span, 0 * 128:0 * 128 + inner] = (folded(dot(slopes_half, keys, TN)) * scaling).astype(BF16)
+        gp[span, 1 * 128:1 * 128 + inner] = (dot(slopes_half, queries, NT) * scaling).astype(BF16)
+        gp[span, 2 * 128:2 * 128 + inner] = dot(soft_half, gates, NT).astype(BF16)
+        gp[span, 3 * 128:3 * 128 + inner] = folded(dot(soft_half, values, TN)).astype(BF16)
 
     def send_pieces(w):
         span = slice(w * TOK, (w + 1) * TOK)
-        out = sum(dot(gp[c, span, :], aw_split[c], NN) for c in range(3))
+        out = dot(gp[span, :3 * 128], aw_split[...], NN)
         for g in range(groups):
             chunk = out[:, g * 128:g * 128 + inner]
             tail = chunk[MAIN:]
@@ -285,8 +296,8 @@
         tail = [got[t * EDGE:(t + 1) * EDGE, inner:] for t in range(inner // third)]
         full = jnp.concatenate([got[:MAIN, :inner], jnp.concatenate(tail, axis=1)], axis=0)
         own_ref[w] = full.astype(BF16)
-        first = jnp.concatenate([full[:EDGE], full[SIDE:SIDE + EDGE]], axis=0)
-        last = jnp.concatenate([full[EDGE:SIDE], full[SIDE + EDGE:]], axis=0)
+        first = jnp.concatenate([full[:rim], full[SIDE:SIDE + rim]], axis=0)
+        last = jnp.concatenate([full[SIDE - rim:SIDE], full[2 * SIDE - rim:]], axis=0)
         if lons <= 2:
             outs = [jnp.where(early, last, first)]
         else:
@@ -318,6 +329,9 @@
                 rows = pl.ds((z * WIN_LON + b) * half + w, WIN_LAT, stride=wins)
                 got = jnp.concatenate([gbias[t, rows, :] for t in range(tiles)], axis=1)
                 right = WIN_LAT * (WIN_LON - 1 - b)
+                if right == 0:
+                    low = low + got
+                    continue
                 low = low + pltpu.roll(jnp.where(place <= b, got, 0.0), right, 1)
                 high = high + pltpu.roll(jnp.where(place > b, got, 0.0), lanes - WIN_LAT * (b + 1), 1)
             for g in range(segs):
@@ -379,14 +393,21 @@
 
     lines = []
     for w in range(wins):
+        if 0 < w == wins - 1:
+            sum_pieces(0)
         window(w)
-        send_pieces(w)
         if w < wins - 1:
+            send_pieces(w)
             lines.append(bias_line(w))
-        if w >= 2:
-            sum_pieces(w - 2)
-
-    grad_w = [dot(gp[c], xs[...], TN) for c in range(3)] + [dot(gp[3], gs[...], TN)]
+        if w == wins - 2:
+            first_rows = slice(0, (wins - 1) * TOK)
+            for c in range(4):
+                w_acc[c] = dot(gp[first_rows, c * 128:c * 128 + inner], (gs if c == 3 else xs)[first_rows, :], TN)
+
+    last_rows = slice((wins - 1) * TOK, wins * TOK)
+    grad_w = [
+        w_acc[c] + dot(gp[last_rows, c * 128:c * 128 + inner], (gs if c == 3 else xs)[last_rows, :], TN) for c in range(4)
+    ]
     rows_w = 4 * inner
     part_w = rows_w // 2
     for c in range(4):
@@ -406,9 +427,9 @@
     core_mate = rows_up[0]
     swap = post_w(w_core.at[1 - keep], w_core_in, core_mate)
 
-    early_span = bias_total(0, wins - 1, lines)
-    early_have, early_out = bias_gather(0, early_span, [lat], [])
-    last_line = bias_line(wins - 1)
+    if wins > 2:
+        sum_pieces(1)
+    send_pieces(wins - 1)
 
     swap.wait_recv()
     sub = part_w // 2
@@ -423,9 +444,6 @@
         w_cur[0, j] = (w_core[keep, part, :].astype(F32) + w_core_in[part, :].astype(F32)).astype(BF16)
         flying[j] = post_w(w_cur.at[0, j], w_in.at[0, j], orders[j][0][1])
 
-    for w in range(max(wins - 2, 0), wins - 1):
-        sum_pieces(w)
-
     def w_step(k):
         for j in range(2):
             flying[j].wait_recv()
@@ -434,18 +452,24 @@
             if k + 1 < steps:
                 flying[j] = post_w(w_cur.at[k + 1, j], w_in.at[k + 1, j], orders[j][k + 1][1])
 
+    last_line = bias_line(wins - 1)
+    early_span = bias_total(0, wins - 1, lines)
+    early_have, early_out = bias_gather(0, early_span, [lat], [])
+
+    order = tail_order(wins, steps, len(gather_order))
     late_have, late_out = [lat], []
-    for i in range(len(gather_order)):
-        if i + 1 < len(gather_order):
-            early_have, early_out = bias_gather(i + 1, early_span, early_have, early_out)
-        if i == 0:
+    late_span = None
+    for task, i in order:
+        if task == "piece":
+            sum_pieces(i)
+        elif task == "w":
+            w_step(i)
+        elif task == "early":
+            early_have, early_out = bias_gather(i, early_span, early_have, early_out)
+        elif task == "sum":
             late_span = bias_total(wins - 1, wins, [last_line])
-        late_have, late_out = bias_gather(i, late_span, late_have, late_out)
-        if i == 0:
-            w_step(0)
-            sum_pieces(wins - 1)
-    for k in range(1, steps):
-        w_step(k)
+        else:
+            late_have, late_out = bias_gather(i, late_span, late_have, late_out)
     both_w = [
         post_w(w_cur.at[steps, j], all_w_ref.at[keep, pl.ds(j * sub, sub)], core_mate) for j in range(2)
     ]
@@ -457,7 +481,8 @@
         copy.wait_send()
 
 
-def block_backward(x, g, aw, ow, table, types, shift):
+def block_backward(reach, unique, x, g, aw, ow, table, types, shift):
+    rim = reach * WIN_LAT
     lats_in, cols, levels, width = x.shape
     inner = aw.shape[1]
     heads, _, rel_total = table.shape
@@ -479,10 +504,10 @@
     hbm = pl.BlockSpec(memory_space=pltpu.HBM)
     dma = pltpu.SemaphoreType.DMA
     return pl.pallas_call(
-        functools.partial(block_kernel, heads),
+        functools.partial(block_kernel, heads, reach),
         out_shape=(
             pltpu.VMEM((wins, TOK, inner), BF16),
-            pltpu.VMEM((sides, wins, 2 * EDGE, inner), BF16),
+            pltpu.VMEM((sides, wins, 2 * rim, inner), BF16),
             pltpu.VMEM((2, 2 * inner, width), BF16),
             pltpu.VMEM((lats, wins * 8, strip), BF16),
         ),
@@ -494,27 +519,28 @@
             pltpu.VMEM(aw.shape, BF16),
             pltpu.VMEM(ow.shape, BF16),
             pltpu.VMEM(table.shape, F32),
-            pltpu.VMEM((2, width // 128, EDGE * levels, 128), F32),
+            pltpu.VMEM((2, width // 128, rim * levels, 128), F32),
             pltpu.VMEM((2, width // 128, SIDE * levels, 128), F32),
-            pltpu.VMEM((sides, wins, 4 * EDGE, width), BF16),
-            pltpu.VMEM((sides, wins, 4 * EDGE, width), BF16),
+            pltpu.VMEM((sides, wins, 4 * rim, width), BF16),
+            pltpu.VMEM((sides, wins, 4 * rim, width), BF16),
             pltpu.VMEM((wins * TOK, width), BF16),
             pltpu.VMEM((wins * TOK, width), BF16),
             pltpu.VMEM((rows, long), F32),
             pltpu.VMEM((heads * WIN_LEVEL * block, 256), F32),
             pltpu.VMEM((tiles, TOK * wins, 128), F32),
             pltpu.VMEM((tiles, TOK * wins, 128), F32),
-            pltpu.VMEM((4, wins * TOK, inner), BF16),
-            pltpu.VMEM((3, inner, groups * 128), BF16),
+            pltpu.VMEM((wins * TOK, 4 * 128), BF16),
+            pltpu.VMEM((3 * 128, groups * 128), BF16),
             pltpu.VMEM((wins, groups, packed, 128), BF16),
             pltpu.VMEM((wins, groups - 1, packed, 128), BF16),
-            pltpu.VMEM((sides, wins, 2 * EDGE, inner), BF16),
+            pltpu.VMEM((sides, wins, 2 * rim, inner), BF16),
             pltpu.VMEM((2, 2 * inner, width), BF16),
             pltpu.VMEM((2 * inner, width), BF16),
             pltpu.VMEM((steps + 1, 2, inner, width), BF16),
             pltpu.VMEM((steps, 2, inner, width), BF16),
             pltpu.VMEM((lon_steps + 1, wins * 8, strip), BF16),
             pltpu.VMEM((lon_steps, wins * 8, strip), BF16),
+            pltpu.VMEM((4, inner, width), F32),
             pltpu.VMEM((quads * 8, 256), F32),
             pltpu.VMEM((up(WIN_LAT * PART, 128) // 128, quads * 8, 128), F32),
             pltpu.VMEM((up(WIN_LAT * PART, 128) // 128, up(quads, 8), 128), F32),
@@ -526,17 +552,18 @@
             dma((2, wins + 2 * (lon_steps - 1) + 2 * (lats - 1))),
         ],
         compiler_params=pltpu.CompilerParams(
-            collective_id=0, has_side_effects=True, vmem_limit_bytes=54 * 1024 * 1024
+            collective_id=unique, has_side_effects=True, vmem_limit_bytes=54 * 1024 * 1024
         ),
         cost_estimate=pl.CostEstimate(flops=10**9, bytes_accessed=10**7, transcendentals=10**6),
     )(shift, types, x, g, aw, ow, table)
 
 
-def finish_kernel(shift_ref, own_ref, edge_ref, w_ref, bias_ref,
+def finish_kernel(reach, shift_ref, own_ref, edge_ref, w_ref, bias_ref,
                   feature_out, aw_out, ow_out, table_out,
                   feature, aw, ow, table, wide, edges, sems):
     shift = shift_ref[0]
     early = shift <= HALF
+    rows = reach * WIN_LAT
     wins = own_ref.shape[0]
     chunk = own_ref.shape[2]
     levels = wins * WIN_LEVEL
@@ -580,12 +607,12 @@
         for z in range(WIN_LEVEL):
             level = WIN_LEVEL * w + z
             wide[pl.ds(level, SIDE, stride=levels), :chunk] = full[z * SIDE:(z + 1) * SIDE]
-            edges[pl.ds(level, EDGE, stride=levels), :chunk] = rim[z * EDGE:(z + 1) * EDGE]
+            edges[pl.ds(level, rows, stride=levels), :chunk] = rim[z * rows:(z + 1) * rows]
     run = WIN_LAT * levels
     for c in range(WIN_LON):
         here = lax.rem(c + WIN_LON - shift, WIN_LON)
-        there = jnp.where(early, jnp.maximum(HALF + c - shift, 0), jnp.maximum(c - shift, 0))
-        there = jnp.minimum(there, HALF - 1)
+        there = jnp.where(early, jnp.maximum(reach + c - shift, 0), jnp.maximum(c - shift, 0))
+        there = jnp.minimum(there, reach - 1)
         local = jnp.where(early, (c >= shift).astype(F32), (c < shift).astype(F32)) > 0.5
         near = wide[pl.ds(pl.multiple_of(here * run, 8), run), :]
         far = edges[pl.ds(pl.multiple_of(there * run, 8), run), :]
@@ -596,7 +623,7 @@
         copy.wait()
 
 
-def finish(own, edge, all_w, all_bias, shift, types, heads, rel_total):
+def finish(reach, own, edge, all_w, all_bias, shift, types, heads, rel_total):
     wins, _, chunk = own.shape
     inner = all_w.shape[1] // 2
     levels = wins * WIN_LEVEL
@@ -608,26 +635,35 @@
         ((heads, types, rel_total), F32),
     )
     return pl.pallas_call(
-        finish_kernel,
+        functools.partial(finish_kernel, reach),
         out_shape=tuple(jax.ShapeDtypeStruct(*out) for out in outs),
         in_specs=[pl.BlockSpec(memory_space=pltpu.SMEM)] + [vmem] * 4,
         out_specs=(pl.BlockSpec(memory_space=pl.ANY),) * 4,
         scratch_shapes=[pltpu.VMEM(*out) for out in outs] + [
             pltpu.VMEM((SIDE * levels, 128), F32),
-            pltpu.VMEM((EDGE * levels, 128), F32),
+            pltpu.VMEM((reach * WIN_LAT * levels, 128), F32),
             pltpu.SemaphoreType.DMA((heads + 3,)),
         ],
         compiler_params=pltpu.CompilerParams(vmem_limit_bytes=20 * 1024 * 1024),
     )(shift, own, edge, all_w, all_bias)
 
 
+REACHES = (HALF,)
+
+
 def per_device(features, attend_weight, output_weight, bias_table, bias_type, window_shift, grad_out):
     x, g = (v.transpose(1, 2, 0, 3) for v in (features, grad_out))
     aw = attend_weight.transpose(0, 2, 1)
     table = bias_table.transpose(1, 0, 2)
-    gathered = block_backward(x, g, aw, output_weight, table, bias_type.T, window_shift)
     types, heads, rel_total = bias_table.shape
-    feature_grad, attend_grad, output_grad, bias_grad = finish(*gathered, window_shift, types, heads, rel_total)
+
+    def run(i, x, g, aw, ow, table, kinds, shift):
+        gathered = block_backward(REACHES[i], i, x, g, aw, ow, table, kinds, shift)
+        return finish(REACHES[i], *gathered, shift, types, heads, rel_total)
+
+    feature_grad, attend_grad, output_grad, bias_grad = run(
+        0, x, g, aw, output_weight, table, bias_type.T, window_shift
+    )
     return (
         feature_grad.transpose(2, 0, 1, 3),
         attend_grad.transpose(0, 2, 1),

time: 34.9 us -> 34.3 us (0.983)
  Pallas kernels: 33.4 us -> 32.9 us
    pallas_call x2, Pallas kernels: 33.4 us -> 32.9 us  [the longest x1 30.8 us: block_backward(): pl.pallas_call(functools.partial(block_kernel, heads, reach), out_shape=(...]
where the time goes in v3:
time: 34.3 us; the launch traced here: 34.1 us
  Pallas kernels  32.9 us (96%)
  between operations  1.29 us (4%)
    pallas_call x1, Pallas kernels, block_backward(): pl.pallas_call(functools.partial(block_kernel, heads, reach), out_shape=(...  30.8 us
    pallas_call x1, Pallas kernels, finish(): pl.pallas_call(functools.partial(finish_kernel, reach), out_shape=tuple((...  2.11 us

profile of v3, /device:TPU:0, one launch (start us, length us, event | category | flops | bytes accessed | tf_op | source)
XLA Modules:
  0.0 34.1 jit_solution(14682925542723386674)
XLA Ops:
  1.3 30.8 %shard_map.102 = (bf16[4,144,96]{2,1,0:T(8,128)(2,1)S(1)}, bf16[1,4,72,96]{3,2,1,0:T(8,128)(2,1)S(1)}, bf16[2,192,384]{2,1,0:T(8,128)(2,1)S(1)}, bf16[4,32,1664]{2,1,0:T(8,128)(2,1)S(1)}) custom-call(s32[1]{0:T(128)S(6)} %copy.11.shift_ref, s32[1,4]{1,0:T(1,128)} %bitcast.12, bf16[6,12,8,384]{3,2,1,0:T(8,128)(2,1)} %bitcast.9, ...), custom_call_target="tpu_custom_call" | custom-call | flops 1000000000 | bytes 10000000 | tf_op jit(solution)/shard_map/pallas_call | solution.py:506
  32.0 2.1 %shard_map.103 = (bf16[6,12,8,96]{3,2,1,0:T(8,128)(2,1)}, f32[3,96,384]{2,1,0:T(8,128)}, f32[96,384]{1,0:T(8,128)}, f32[3,64,3312]{2,1,0:T(8,128)}) custom-call(s32[1]{0:T(128)S(6)} %copy.11.shift_ref, bf16[4,144,96]{2,1,0:T(8,128)(2,1)S(1)} %get-tuple-element.12.own_ref, bf16[1,4,72,96]{3,2,1,0:T(8,128)(2,1)S(1)} %get-tuple-element.13.edge_ref, ...), custom_call_target="tpu_custom_call" | custom-call | tf_op jit(solution)/shard_map/pallas_call | solution.py:637

commit v4 on v3

--- a/solution.py
+++ b/solution.py
@@ -64,22 +64,20 @@
 
 
 def tail_order(wins, steps, gathers):
-    tasks = [("piece", w) for w in range(2, wins - 1)]
+    tasks = [("piece", w) for w in range(1, wins - 1)]
     tasks += [("w", 0), ("sum", 0), ("late", 0)] + [("early", i) for i in range(1, gathers)]
     tasks += [("piece", wins - 1)] + [("w", k) for k in range(1, steps)] + [("late", i) for i in range(1, gathers)]
     return tasks
 
 
-def block_kernel(heads, reach, shift_ref, type_ref, x_hbm, g_hbm, aw_hbm, ow_hbm, table_hbm,
+def block_kernel(heads, reach, shift_hbm, type_hbm, x_hbm, g_hbm, aw_hbm, ow_hbm, table_hbm,
                  own_ref, edge_ref, all_w_ref, all_bias_ref,
                  x_own, g_own, aw, ow, table, halo_f, own_f, halo_out, halo_in, xs, gs,
                  line, parts, bias, gbias, gp, aw_split, piece_out, piece_in, edge_out,
                  w_core, w_core_in, w_cur, w_in, bias_cur, bias_in, w_acc, folds, spots_f, rows_f,
-                 local, halo_sem, piece_sem, edge_sem, w_sem, bias_sem):
+                 shift_ref, type_ref, local, halo_sem, piece_sem, edge_sem, w_sem, bias_sem):
     lons, lats, groups = (lax.axis_size(name) for name in ("lon", "lat", "head"))
     lon, lat, head = (lax.axis_index(name) for name in ("lon", "lat", "head"))
-    shift = shift_ref[0]
-    early = shift <= HALF
     rim = reach * WIN_LAT
     cols, levels, width = x_own.shape[1:]
     wins = levels // WIN_LEVEL
@@ -92,10 +90,13 @@
     loads = [
         pltpu.make_async_copy(src, dst, local.at[i])
         for i, (src, dst) in enumerate(
-            ((x_hbm, x_own), (g_hbm, g_own), (table_hbm, table), (aw_hbm, aw), (ow_hbm, ow))
+            (
+                (x_hbm, x_own), (g_hbm, g_own), (table_hbm, table), (aw_hbm, aw), (ow_hbm, ow),
+                (type_hbm, type_ref), (shift_hbm, shift_ref),
+            )
         )
     ]
-    for load in loads:
+    for load in loads[-1:] + loads[:-1]:
         load.start()
 
     east = (lax.rem(lon + 1, lons), lat, head)
@@ -127,6 +128,9 @@
         rows = pl.ds(level, count, stride=levels)
         return jnp.concatenate([src[i, t, rows, :] for t in range(strips)], axis=1)
 
+    loads[6].wait()
+    shift = shift_ref[0]
+    early = shift <= HALF
     loads[0].wait()
     loads[1].wait()
     sent = []
@@ -158,6 +162,7 @@
                 put(own_f, i, b * WIN_LAT + a, src[a, col])
 
     loads[2].wait()
+    loads[5].wait()
     parts[...] = jnp.zeros_like(parts)
     for h in range(heads):
         for w in range(wins):
@@ -393,8 +398,6 @@
 
     lines = []
     for w in range(wins):
-        if 0 < w == wins - 1:
-            sum_pieces(0)
         window(w)
         if w < wins - 1:
             send_pieces(w)
@@ -427,8 +430,8 @@
     core_mate = rows_up[0]
     swap = post_w(w_core.at[1 - keep], w_core_in, core_mate)
 
-    if wins > 2:
-        sum_pieces(1)
+    if wins > 1:
+        sum_pieces(0)
     send_pieces(wins - 1)
 
     swap.wait_recv()
@@ -500,7 +503,6 @@
     strip = up(rel_total, 256) // 2
     quads = heads * WIN_LEVEL * WIN_LEVEL
     vmem = pl.BlockSpec(memory_space=pltpu.VMEM)
-    smem = pl.BlockSpec(memory_space=pltpu.SMEM)
     hbm = pl.BlockSpec(memory_space=pltpu.HBM)
     dma = pltpu.SemaphoreType.DMA
     return pl.pallas_call(
@@ -511,7 +513,7 @@
             pltpu.VMEM((2, 2 * inner, width), BF16),
             pltpu.VMEM((lats, wins * 8, strip), BF16),
         ),
-        in_specs=[smem, smem] + [hbm] * 5,
+        in_specs=[hbm] * 7,
         out_specs=(vmem,) * 4,
         scratch_shapes=[
             pltpu.VMEM(x.shape, BF16),
@@ -544,7 +546,9 @@
             pltpu.VMEM((quads * 8, 256), F32),
             pltpu.VMEM((up(WIN_LAT * PART, 128) // 128, quads * 8, 128), F32),
             pltpu.VMEM((up(WIN_LAT * PART, 128) // 128, up(quads, 8), 128), F32),
-            dma((5,)),
+            pltpu.SMEM(shift.shape, jnp.int32),
+            pltpu.SMEM(types.shape, jnp.int32),
+            dma((7,)),
             dma((2, wins * sides)),
             dma((2, wins * (groups - 1))),
             dma((2, wins * sides)),
@@ -558,11 +562,11 @@
     )(shift, types, x, g, aw, ow, table)
 
 
-def finish_kernel(reach, shift_ref, own_ref, edge_ref, w_ref, bias_ref,
+def finish_kernel(reach, shift_hbm, own_ref, edge_ref, w_ref, bias_ref,
                   feature_out, aw_out, ow_out, table_out,
-                  feature, aw, ow, table, wide, edges, sems):
-    shift = shift_ref[0]
-    early = shift <= HALF
+                  feature, aw, ow, table, wide, edges, shift_ref, shift_sem, sems):
+    shift_copy = pltpu.make_async_copy(shift_hbm, shift_ref, shift_sem)
+    shift_copy.start()
     rows = reach * WIN_LAT
     wins = own_ref.shape[0]
     chunk = own_ref.shape[2]
@@ -597,6 +601,10 @@
     ow[...] = flat[3 * inner:].astype(F32)
     put(aw, aw_out)
     put(ow, ow_out)
+
+    shift_copy.wait()
+    shift = shift_ref[0]
+    early = shift <= HALF
 
     for w in range(wins):
         full = own_ref[w].astype(F32)
@@ -637,11 +645,13 @@
     return pl.pallas_call(
         functools.partial(finish_kernel, reach),
         out_shape=tuple(jax.ShapeDtypeStruct(*out) for out in outs),
-        in_specs=[pl.BlockSpec(memory_space=pltpu.SMEM)] + [vmem] * 4,
+        in_specs=[pl.BlockSpec(memory_space=pl.ANY)] + [vmem] * 4,
         out_specs=(pl.BlockSpec(memory_space=pl.ANY),) * 4,
         scratch_shapes=[pltpu.VMEM(*out) for out in outs] + [
             pltpu.VMEM((SIDE * levels, 128), F32),
             pltpu.VMEM((reach * WIN_LAT * levels, 128), F32),
+            pltpu.SMEM(shift.shape, jnp.int32),
+            pltpu.SemaphoreType.DMA,
             pltpu.SemaphoreType.DMA((heads + 3,)),
         ],
         compiler_params=pltpu.CompilerParams(vmem_limit_bytes=20 * 1024 * 1024),

time: 34.3 us -> 33.5 us (0.977)
  Pallas kernels: 32.9 us -> 32.1 us
    pallas_call x1, Pallas kernels: 30.8 us -> 30 us  [block_backward(): pl.pallas_call(functools.partial(block_kernel, heads, reach), out_shape=(...]
where the time goes in v4:
time: 33.5 us; the launch traced here: 33.4 us
  Pallas kernels  32.1 us (96%)
  between operations  1.29 us (4%)
    pallas_call x1, Pallas kernels, block_backward(): pl.pallas_call(functools.partial(block_kernel, heads, reach), out_shape=(...  30 us
    pallas_call x1, Pallas kernels, finish(): pl.pallas_call(functools.partial(finish_kernel, reach), out_shape=tuple((...  2.08 us

profile of v4, /device:TPU:0, one launch (start us, length us, event | category | flops | bytes accessed | tf_op | source)
XLA Modules:
  0.0 33.4 jit_solution(14014151954162236169)
XLA Ops:
  1.3 30.0 %shard_map.102 = (bf16[4,144,96]{2,1,0:T(8,128)(2,1)S(1)}, bf16[1,4,72,96]{3,2,1,0:T(8,128)(2,1)S(1)}, bf16[2,192,384]{2,1,0:T(8,128)(2,1)S(1)}, bf16[4,32,1664]{2,1,0:T(8,128)(2,1)S(1)}) custom-call(s32[1]{0:T(128)S(6)} %copy.11.shift_hbm, s32[1,4]{1,0:T(1,128)} %bitcast.12, bf16[6,12,8,384]{3,2,1,0:T(8,128)(2,1)} %bitcast.9, ...), custom_call_target="tpu_custom_call" | custom-call | flops 1000000000 | bytes 10000000 | tf_op jit(solution)/shard_map/pallas_call | solution.py:508
  31.3 2.1 %shard_map.103 = (bf16[6,12,8,96]{3,2,1,0:T(8,128)(2,1)}, f32[3,96,384]{2,1,0:T(8,128)}, f32[96,384]{1,0:T(8,128)}, f32[3,64,3312]{2,1,0:T(8,128)}) custom-call(s32[1]{0:T(128)S(6)} %copy.11.shift_hbm, bf16[4,144,96]{2,1,0:T(8,128)(2,1)S(1)} %get-tuple-element.12.own_ref, bf16[1,4,72,96]{3,2,1,0:T(8,128)(2,1)S(1)} %get-tuple-element.13.edge_ref, ...), custom_call_target="tpu_custom_call" | custom-call | tf_op jit(solution)/shard_map/pallas_call | solution.py:645

commit v5 on v4

--- a/solution.py
+++ b/solution.py
@@ -131,11 +131,11 @@
     loads[6].wait()
     shift = shift_ref[0]
     early = shift <= HALF
-    loads[0].wait()
-    loads[1].wait()
     sent = []
     for n in range(len(sides)):
         for i, src in enumerate((x_own, g_own)):
+            if n == 0:
+                loads[i].wait()
             for b in range(reach):
                 low = jnp.maximum(shift + b - reach, 0)
                 high = jnp.minimum(shift + b, cols - 1)

time: 33.5 us -> 33.5 us (level)
  no operation moved by 1% of the time
where the time goes in v5:
time: 33.5 us; the launch traced here: 33.4 us
  Pallas kernels  32.1 us (96%)
  between operations  1.29 us (4%)
    pallas_call x1, Pallas kernels, block_backward(): pl.pallas_call(functools.partial(block_kernel, heads, reach), out_shape=(...  30 us
    pallas_call x1, Pallas kernels, finish(): pl.pallas_call(functools.partial(finish_kernel, reach), out_shape=tuple((...  2.08 us

profile of v5, /device:TPU:0, one launch (start us, length us, event | category | flops | bytes accessed | tf_op | source)
XLA Modules:
  0.0 33.4 jit_solution(18278046311967561716)
XLA Ops:
  1.3 30.0 %shard_map.102 = (bf16[4,144,96]{2,1,0:T(8,128)(2,1)S(1)}, bf16[1,4,72,96]{3,2,1,0:T(8,128)(2,1)S(1)}, bf16[2,192,384]{2,1,0:T(8,128)(2,1)S(1)}, bf16[4,32,1664]{2,1,0:T(8,128)(2,1)S(1)}) custom-call(s32[1]{0:T(128)S(6)} %copy.11.shift_hbm, s32[1,4]{1,0:T(1,128)} %bitcast.12, bf16[6,12,8,384]{3,2,1,0:T(8,128)(2,1)} %bitcast.9, ...), custom_call_target="tpu_custom_call" | custom-call | flops 1000000000 | bytes 10000000 | tf_op jit(solution)/shard_map/pallas_call | solution.py:508
  31.3 2.1 %shard_map.103 = (bf16[6,12,8,96]{3,2,1,0:T(8,128)(2,1)}, f32[3,96,384]{2,1,0:T(8,128)}, f32[96,384]{1,0:T(8,128)}, f32[3,64,3312]{2,1,0:T(8,128)}) custom-call(s32[1]{0:T(128)S(6)} %copy.11.shift_hbm, bf16[4,144,96]{2,1,0:T(8,128)(2,1)S(1)} %get-tuple-element.12.own_ref, bf16[1,4,72,96]{3,2,1,0:T(8,128)(2,1)S(1)} %get-tuple-element.13.edge_ref, ...), custom_call_target="tpu_custom_call" | custom-call | tf_op jit(solution)/shard_map/pallas_call | solution.py:645
